TPU v7x, 32 devices: a whole 2x2x4 slice. The times are simulated.
32 devices in a mesh: seq: 4 (over y, x), exp: 8 (over z, core).
Axes of the slice: x: 2, y: 2, z: 4, core: 2. Of those that a mesh axis runs over, the one named last changes fastest.
Arguments:
- tokens: bfloat16 [2, 24576, 1024], P(None, ('seq', 'exp')), may hold values from -60 to 60
- router: bfloat16 [1024, 64], replicated, may hold values from -0.25 to 0.25
- w_in: bfloat16 [16, 1024, 4096], P('exp', None, 'seq'), may hold values from -0.1875 to 0.1875
- w_out: bfloat16 [16, 4096, 1024], P('exp', 'seq'), may hold values from -0.09375 to 0.09375
- grad_out: bfloat16 [2, 24576, 1024], P(None, ('seq', 'exp')), may hold values from -6 to 6
Outputs:
- mixed: bfloat16 [2, 24576, 1024], P(None, ('seq', 'exp'))
- grad_tokens: bfloat16 [2, 24576, 1024], P(None, ('seq', 'exp'))
- grad_router: float32 [1024, 64], P(('seq', 'exp'))
- grad_w_in: bfloat16 [16, 1024, 4096], P('exp', None, 'seq')
- grad_w_out: bfloat16 [16, 4096, 1024], P('exp', 'seq')
All inputs are finite; a program needn't handle non-finite values.
Results may differ from a plain program's by a relative error of at most 0.018.
Values may be sent and summed in bfloat16 or wider, within the bound.
A program may use at most 128 MiB of HBM per device.

v0:
```python
import functools

import jax
import jax.numpy as jnp
from jax import lax
from jax.experimental import pallas as pl
from jax.experimental.pallas import tpu as pltpu
from jax.sharding import PartitionSpec as P

MESH = pl.DeviceIdType.MESH
F32 = jnp.float32
BF16 = jnp.bfloat16
NT = (((1,), (1,)), ((), ()))


def dot(a, b):
    return jnp.dot(a, b, preferred_element_type=F32)


def dot_nt(a, b):
    return lax.dot_general(a, b, NT, preferred_element_type=F32)


def place(seq_n, exp_n):
    s = lax.axis_index("seq")
    e = lax.axis_index("exp")
    h, par = e // 2, e % 2
    pair = (s, h * 2 + (1 - par))
    seq_peers = [((s + k) % seq_n, e) for k in range(1, seq_n)]
    exp_peers = [(s, ((h + k) % (exp_n // 2)) * 2 + par) for k in range(1, exp_n // 2)]
    return s, h, par, pair, seq_peers, exp_peers


def greet(peers):
    barrier = pltpu.get_barrier_semaphore()
    for peer in peers:
        pl.semaphore_signal(barrier, inc=1, device_id=peer, device_id_type=MESH)


def await_greetings(peers):
    pl.semaphore_wait(pltpu.get_barrier_semaphore(), len(peers))


class Sender:
    def __init__(self, send_sem, recv_sem):
        self.send_sem, self.recv_sem, self.count, self.open = send_sem, recv_sem, 0, []

    def start(self, src, dst, peer):
        copy = pltpu.make_async_remote_copy(
            src_ref=src,
            dst_ref=dst,
            send_sem=self.send_sem.at[self.count],
            recv_sem=self.recv_sem.at[self.count],
            device_id=peer,
            device_id_type=MESH,
        )
        copy.start()
        self.count += 1
        self.open.append(copy)
        return copy

    def drain(self):
        for copy in self.open:
            copy.wait_send()


def front_copies(seq_n, exp_n):
    half = exp_n // 2
    seq, rest = seq_n - 1, half - 1
    stats = 1 + seq + rest
    gather = rest + half * seq + seq_n
    return stats + 2 * (stats + seq) + 2 * seq + 3 * gather


def as_row(column, n):
    eye = lax.broadcasted_iota(jnp.int32, (n, n), 0) == lax.broadcasted_iota(jnp.int32, (n, n), 1)
    return jnp.sum(jnp.where(eye, jnp.broadcast_to(column, (n, n)), 0.0), axis=0, keepdims=True)


def row_softmax(lg):
    q = jnp.exp(lg - jnp.max(lg, axis=1, keepdims=True))
    return q / jnp.sum(q, axis=1, keepdims=True)


def front(
    seq_n, exp_n, tok_hbm, rt, gout_hbm, win_hbm, wout_hbm,
    so_o, wr_o, st_o, x_o, g_o, hid_o, pg_o,
    tok, gout, win, wout, xt, qt, st_a, st_p, st_b, st_s, st_c, st_z,
    buf_a, rcv_a, buf_b, rcv_b, buf_c, rcv_c, xf, xg, buf_e, rcv_e, ag, inn, fac_a, fac_b, fac_c,
    w_sem, send_sem, recv_sem,
):
    clips, rows, width = tok.shape
    slots = rt.shape[0]
    half = exp_n // 2
    owned = slots // exp_n
    dc = width // seq_n
    n_rows = clips * owned
    experts = win.shape[0]
    s, h, par, pair, seq_peers, exp_peers = place(seq_n, exp_n)

    load_tok = [pltpu.make_async_copy(tok_hbm.at[c], tok.at[c], w_sem.at[c]) for c in range(clips)]
    load_gout = [
        pltpu.make_async_copy(gout_hbm.at[c], gout.at[c], w_sem.at[clips + c]) for c in range(clips)
    ]
    load_in = pltpu.make_async_copy(win_hbm, win, w_sem.at[2 * clips])
    load_out = pltpu.make_async_copy(wout_hbm, wout, w_sem.at[2 * clips + 1])
    for load in load_tok + load_gout:
        load.start()
    greet([pair] + seq_peers + exp_peers)
    net = Sender(send_sem, recv_sem)

    peaks, masses = [], []
    for c in range(clips):
        load_tok[c].wait()
        lg = dot_nt(tok[c], rt[...])
        m = jnp.max(lg, axis=0, keepdims=True)
        p = jnp.exp(lg - m)
        peaks.append(m)
        masses.append(jnp.sum(p, axis=0, keepdims=True))
        xt[c] = p.T.astype(BF16)
        qt[c] = row_softmax(lg).T.astype(BF16)
    pad = jnp.zeros((8 - 2 * clips, slots), F32)
    st_a[...] = jnp.concatenate(peaks + masses + [pad], axis=0)

    def combine(parts):
        m = parts[0][:clips]
        for part in parts[1:]:
            m = jnp.maximum(m, part[:clips])
        mass = None
        for part in parts:
            term = part[clips : 2 * clips] * jnp.exp(part[:clips] - m)
            mass = term if mass is None else mass + term
        return jnp.concatenate([m, mass, pad], axis=0)

    def lay_out(value, kind, c):
        for t in range(seq_n):
            block = value[:, t * dc : (t + 1) * dc].reshape(half, 2, owned, dc).astype(BF16)
            for q in range(2):
                buf_a[kind, q, :, t, c] = block[:, q]

    def arrived(copies):
        for copy in copies:
            copy.wait_recv()

    def total_of(own, parts, count):
        total = own.astype(F32)
        for k in range(count):
            total = total + parts[k].astype(F32)
        return total

    def to_pair(kind):
        return [net.start(buf_a.at[kind, 1 - par], rcv_a.at[kind], pair)]

    def factors(ref, tiles, joint, norm=None):
        terms = [jnp.exp(tile[:clips] - joint[:clips]) for tile in tiles]
        if norm is not None:
            terms = [term / norm for term in terms]
        spare = ref.shape[3] - clips * len(tiles)
        if spare:
            terms.append(jnp.zeros((spare, slots), F32))
        columns = jnp.concatenate(terms, axis=0).T.reshape(half, 2, owned, ref.shape[3])
        for q in range(2):
            ref[q] = columns[:, q]

    def to_seq(kind):
        if kind == 0:
            factors(fac_a, [st_a[...], st_p[...]], st_b[...])
            fac = fac_a[par]
        for t in range(seq_n):
            for c in range(clips):
                mine = buf_a[kind, par, :, t, c].astype(F32)
                other = rcv_a[kind, :, t, c].astype(F32)
                if kind == 0:
                    mine = mine * fac[:, :, c : c + 1]
                    other = other * fac[:, :, clips + c : clips + c + 1]
                buf_b[kind, t, :, c] = (mine + other).astype(BF16)
        return [
            net.start(buf_b.at[kind, peer[0]], rcv_b.at[kind, k], peer)
            for k, peer in enumerate(seq_peers)
        ]

    def to_exp(kind):
        if kind == 0:
            factors(fac_b, [st_b[...]] + [st_s[k] for k in range(seq_n - 1)], st_c[...])
            fac = fac_b[par]
        for c in range(clips):
            total = buf_b[kind, s, :, c].astype(F32)
            if kind == 0:
                total = total * fac[:, :, c : c + 1]
            for k in range(seq_n - 1):
                part = rcv_b[kind, k, :, c].astype(F32)
                if kind == 0:
                    at = (k + 1) * clips + c
                    part = part * fac[:, :, at : at + 1]
                total = total + part
            buf_c[kind, :, c] = total.astype(BF16)
        return [
            net.start(buf_c.at[kind, (h + 1 + k) % half], rcv_c.at[kind, k], peer)
            for k, peer in enumerate(exp_peers)
        ]

    def to_group(kind):
        if kind == 0:
            tiles = [st_c[...]] + [st_z[k] for k in range(half - 1)]
            factors(fac_c, tiles, stats, stats[clips : 2 * clips])
            fac = fac_c[par, h]
        for c in range(clips):
            total = buf_c[kind, h, c].astype(F32)
            if kind == 0:
                total = total * fac[:, c : c + 1]
            for k in range(half - 1):
                part = rcv_c[kind, k, c].astype(F32)
                if kind == 0:
                    at = (k + 1) * clips + c
                    part = part * fac[:, at : at + 1]
                total = total + part
            if kind == 0:
                xf[c] = total
            xg[kind, s, c] = total.astype(BF16)
        return [net.start(xg.at[kind, s], xg.at[kind, s], peer) for peer in seq_peers]

    def rows_of(kind):
        return jnp.concatenate(
            [xg[kind, t].astype(F32).reshape(n_rows, dc) for t in range(seq_n)], axis=1
        )

    await_greetings([pair] + seq_peers + exp_peers)
    stat = [net.start(st_a, st_p, pair)]
    for c in range(clips):
        lay_out(dot(xt[c], tok[c]), 0, c)
    inputs = to_pair(0)
    load_gout[0].wait()
    lay_out(dot(qt[0], gout[0]), 1, 0)
    arrived(stat)
    st_b[...] = combine([st_a[...], st_p[...]])
    stat = [net.start(st_b, st_s.at[k], peer) for k, peer in enumerate(seq_peers)]
    arrived(inputs)
    inputs = to_seq(0)
    for c in range(1, clips):
        load_gout[c].wait()
        lay_out(dot(qt[c], gout[c]), 1, c)
    load_in.start()
    load_out.start()
    grads = to_pair(1)
    arrived(stat)
    st_c[...] = combine([st_b[...]] + [st_s[k] for k in range(seq_n - 1)])
    stat = [net.start(st_c, st_z.at[k], peer) for k, peer in enumerate(exp_peers)]
    arrived(grads)
    grads = to_seq(1)
    arrived(inputs)
    inputs = to_exp(0)
    arrived(grads)
    grads = to_exp(1)
    arrived(stat)
    stats = combine([st_c[...]] + [st_z[k] for k in range(half - 1)])
    arrived(inputs)
    inputs = to_group(0)
    arrived(grads)
    grads = to_group(1)

    row = lax.broadcasted_iota(jnp.int32, (n_rows, 1), 0)
    expert_of = (row % owned) // (owned // experts)
    mask = [(expert_of == e).astype(F32) for e in range(experts)]
    load_in.wait()
    load_out.wait()
    arrived(inputs)
    x_rows = rows_of(0)
    pre = 0.0
    for e in range(experts):
        mine = x_rows * mask[e]
        x_o[e] = mine
        pre = pre + dot(mine.astype(BF16), win[e])
    hidden, back = jax.vjp(jax.nn.gelu, pre)

    def share(kind, part):
        for t in range(seq_n):
            cut = slice(t * dc, (t + 1) * dc)
            buf_e[kind, t] = part[:, cut].reshape(clips, owned, dc).astype(BF16)
        return [
            net.start(buf_e.at[kind, peer[0]], rcv_e.at[kind, k], peer)
            for k, peer in enumerate(seq_peers)
        ]

    out_part = 0.0
    for e in range(experts):
        mine = hidden * mask[e]
        hid_o[e] = mine
        out_part = out_part + dot(mine.astype(BF16), wout[e])
    forward = share(0, out_part)

    def send_piece(kind, peers, g, t):
        copies = []
        for peer in peers:
            at = ag.at[kind, par, g, t]
            copies.append([net.start(at, at, peer)])
            if kind == 1:
                at = inn.at[par, g, t]
                copies[-1].append(net.start(at, at, peer))
        return copies

    def send_column(kind, t):
        at = ag.at[kind, par, :, t]
        copies = [net.start(at, at, pair)]
        if kind == 1:
            at = inn.at[par, :, t]
            copies.append(net.start(at, at, pair))
        return copies

    def make_piece(kind):
        piece = total_of(buf_e[kind, s], rcv_e.at[kind], seq_n - 1).astype(BF16)
        ag[kind, par, h, s] = piece
        if kind == 1:
            inner = jnp.sum(piece.astype(F32) * xf[...], axis=2, keepdims=True)
            lane = lax.broadcasted_iota(jnp.int32, inn.shape[3:], 1)
            tile = jnp.zeros(inn.shape[3:], F32)
            for c in range(clips):
                tile = jnp.where(lane == c, inner[c], tile)
            inn[par, h, s] = tile
        along[kind] = send_piece(kind, exp_peers, h, s)
        across[kind] = [send_piece(kind, seq_peers, h, s)]

    owners = [(q, g) for g in range(half) for q in range(2)]

    def write_out(kind):
        for c in range(clips):
            for t in range(seq_n):
                cut = slice(t * dc, (t + 1) * dc)
                value = jnp.concatenate(
                    [ag[kind, q, g, t, c].astype(F32) for q, g in owners], axis=0
                ).astype(BF16)
                if kind == 0:
                    so_o[c, :, cut] = value
                else:
                    wr_o[c, slots:, cut] = value

    along, across, last = {}, {}, {}
    arrived(grads)
    g_rows = rows_of(1).astype(BF16)
    g_o[...] = g_rows
    hidden_grad = 0.0
    for e in range(experts):
        hidden_grad = hidden_grad + dot_nt(g_rows, wout[e]) * mask[e]
    arrived(forward)
    make_piece(0)
    pre_grad = back(hidden_grad)[0]
    in_part = 0.0
    for e in range(experts):
        in_part = in_part + dot_nt((pre_grad * mask[e]).astype(BF16), win[e])
    backward = share(1, in_part)
    pg_o[...] = pre_grad.astype(BF16)
    for c in range(clips):
        wr_o[c, :slots] = rt[...]
    for k in range(half - 1):
        arrived(along[0][k])
        across[0].append(send_piece(0, seq_peers, (h + half - 1 - k) % half, s))
    arrived(backward)
    make_piece(1)
    for k in range(half - 1):
        arrived(along[1][k])
        across[1].append(send_piece(1, seq_peers, (h + half - 1 - k) % half, s))
    for kind in (0, 1):
        last[kind] = send_column(kind, s)
    for k in range(seq_n - 1):
        source = (s + seq_n - 1 - k) % seq_n
        for kind in (0, 1):
            for step in across[kind]:
                arrived(step[k])
            last[kind] += send_column(kind, source)
    backward, forward = last[1], last[0]
    arrived(forward)
    write_out(0)
    arrived(backward)
    write_out(1)
    parts = []
    for q, g in owners:
        part = inn[q, g, 0]
        for t in range(1, seq_n):
            part = part + inn[q, g, t]
        parts.append(part)
    inners = jnp.concatenate(parts, axis=0)
    inners = [as_row(inners[:, c : c + 1], slots) for c in range(clips)]
    st_o[...] = jnp.concatenate(
        [stats[: 2 * clips]] + inners + [jnp.zeros((8 - 3 * clips, slots), F32)], axis=0
    )
    net.drain()


def finish(clips, steps, tok, gout, so, wr, st, x, g, hid, pg, mixed, gt, gr, gwin, gwout):
    i = pl.program_id(0)
    c = i // (steps // clips)
    slots = so.shape[1]
    peak = st[pl.ds(c, 1), :]
    mass = st[pl.ds(clips + c, 1), :]
    inner = st[pl.ds(2 * clips + c, 1), :]
    t, go = tok[0], gout[0]
    both = dot_nt(t, wr[0])
    lg, dispatch_grad = both[:, :slots], both[:, slots:]
    mixing_grad = dot_nt(go, so[0])
    dispatch = jnp.exp(lg - peak) / mass
    mixing = row_softmax(lg)
    lgrad = dispatch * (dispatch_grad - inner) + mixing * (
        mixing_grad - jnp.sum(mixing * mixing_grad, axis=1, keepdims=True)
    )
    mixed[0] = dot(mixing.astype(BF16), so[0]).astype(BF16)
    gt[0] = dot(jnp.concatenate([lgrad, dispatch], axis=1).astype(BF16), wr[0]).astype(BF16)

    @pl.when(i == 0)
    def _():
        gr[...] = jnp.zeros_like(gr)

    gr[...] += dot(lgrad.T.astype(BF16), t)
    gwin[0] = dot(x[0].T.astype(BF16), pg[...]).astype(BF16)
    gwout[0] = dot(hid[0].T.astype(BF16), g[...]).astype(BF16)


def scatter(seq_n, exp_n, gr, out, buf_a, rcv_a, buf_b, rcv_b, send_sem, recv_sem):
    half = exp_n // 2
    s, h, par, pair, _, _ = place(seq_n, exp_n)
    ways = [(a, b) for a in range(seq_n) for b in range(half) if a or b]
    there = [((s + a) % seq_n, (h + b) % half) for a, b in ways]
    peers = [(t, g * 2 + par) for t, g in there]
    rows, slots = out.shape
    packed = buf_b.shape[2]
    pack = rows // packed
    greet([pair] + peers)
    net = Sender(send_sem, recv_sem)
    whole = gr[...].T
    for t in range(seq_n):
        for g in range(half):
            for q in range(2):
                at = (t * exp_n + 2 * g + q) * rows
                parts = [whole[at + j * packed : at + (j + 1) * packed] for j in range(pack)]
                buf_a[q, t, g] = jnp.concatenate(parts, axis=1).astype(BF16)
    await_greetings([pair] + peers)
    net.start(buf_a.at[1 - par], rcv_a, pair).wait_recv()
    buf_b[...] = (buf_a[par].astype(F32) + rcv_a[...].astype(F32)).astype(BF16)
    copies = [
        net.start(buf_b.at[t, g], rcv_b.at[k], peers[k]) for k, (t, g) in enumerate(there)
    ]
    total = buf_b[s, h].astype(F32)
    for k, copy in enumerate(copies):
        copy.wait_recv()
        total = total + rcv_b[k].astype(F32)
    for j in range(pack):
        out[j * packed : (j + 1) * packed] = total[:, j * slots : (j + 1) * slots]
    net.drain()


def on_device(seq_n, exp_n, tokens, router, w_in, w_out, grad_out):
    clips, rows, width = tokens.shape
    slots = router.shape[1]
    experts, _, ff = w_in.shape
    half = exp_n // 2
    owned = slots // exp_n
    dc = width // seq_n
    n_rows = clips * owned
    router_t = router.T
    vmem = pl.BlockSpec(memory_space=pltpu.VMEM)
    hbm = pl.BlockSpec(memory_space=pltpu.HBM)
    shape = jax.ShapeDtypeStruct
    block = (clips, owned, dc)
    n_front = front_copies(seq_n, exp_n)
    so, wr, st, x, g, hid, pg = pl.pallas_call(
        functools.partial(front, seq_n, exp_n),
        out_shape=(
            shape((clips, slots, width), BF16),
            shape((clips, 2 * slots, width), BF16),
            shape((8, slots), F32),
            shape((experts, n_rows, width), F32),
            shape((n_rows, width), BF16),
            shape((experts, n_rows, ff), F32),
            shape((n_rows, ff), BF16),
        ),
        in_specs=[hbm, vmem, hbm, hbm, hbm],
        out_specs=(vmem,) * 7,
        scratch_shapes=[
            pltpu.VMEM(tokens.shape, BF16),
            pltpu.VMEM(tokens.shape, BF16),
            pltpu.VMEM(w_in.shape, BF16),
            pltpu.VMEM(w_out.shape, BF16),
            pltpu.VMEM((clips, slots, rows), BF16),
            pltpu.VMEM((clips, slots, rows), BF16),
            pltpu.VMEM((8, slots), F32),
            pltpu.VMEM((8, slots), F32),
            pltpu.VMEM((8, slots), F32),
            pltpu.VMEM((seq_n - 1, 8, slots), F32),
            pltpu.VMEM((8, slots), F32),
            pltpu.VMEM((half - 1, 8, slots), F32),
            pltpu.VMEM((2, 2, half, seq_n) + block, BF16),
            pltpu.VMEM((2, half, seq_n) + block, BF16),
            pltpu.VMEM((2, seq_n, half) + block, BF16),
            pltpu.VMEM((2, seq_n - 1, half) + block, BF16),
            pltpu.VMEM((2, half) + block, BF16),
            pltpu.VMEM((2, half - 1) + block, BF16),
            pltpu.VMEM(block, F32),
            pltpu.VMEM((2, seq_n) + block, BF16),
            pltpu.VMEM((2, seq_n) + block, BF16),
            pltpu.VMEM((2, seq_n - 1) + block, BF16),
            pltpu.VMEM((2, 2, half, seq_n) + block, BF16),
            pltpu.VMEM((2, half, seq_n, owned, 128), F32),
            pltpu.VMEM((2, half, owned, -(-2 * clips // 8) * 8), F32),
            pltpu.VMEM((2, half, owned, -(-seq_n * clips // 8) * 8), F32),
            pltpu.VMEM((2, half, owned, -(-half * clips // 8) * 8), F32),
            pltpu.SemaphoreType.DMA((2 * clips + 2,)),
            pltpu.SemaphoreType.DMA((n_front,)),
            pltpu.SemaphoreType.DMA((n_front,)),
        ],
        compiler_params=pltpu.CompilerParams(collective_id=0, has_side_effects=True),
        name="front",
    )(tokens, router_t, grad_out, w_in, w_out)

    steps = 2 * clips
    t_blocks = steps // clips
    w_blocks = steps // experts
    token_spec = pl.BlockSpec((1, rows // t_blocks, width), lambda i: (i // t_blocks, i % t_blocks, 0))

    def slot_spec(a):
        return pl.BlockSpec((1,) + a.shape[1:], lambda i: (i // t_blocks, 0, 0))

    def fixed(a):
        return pl.BlockSpec(a.shape, lambda i: (0,) * a.ndim)

    mixed, grad_tokens, gr, grad_w_in, grad_w_out = pl.pallas_call(
        functools.partial(finish, clips, steps),
        grid=(steps,),
        out_shape=(
            shape(tokens.shape, BF16),
            shape(tokens.shape, BF16),
            shape((slots, width), F32),
            shape(w_in.shape, BF16),
            shape(w_out.shape, BF16),
        ),
        in_specs=[
            token_spec,
            token_spec,
            slot_spec(so),
            slot_spec(wr),
            fixed(st),
            pl.BlockSpec((1, n_rows, width // w_blocks), lambda i: (i // w_blocks, 0, i % w_blocks)),
            fixed(g),
            pl.BlockSpec((1, n_rows, ff // w_blocks), lambda i: (i // w_blocks, 0, i % w_blocks)),
            fixed(pg),
        ],
        out_specs=(
            token_spec,
            token_spec,
            pl.BlockSpec((slots, width), lambda i: (0, 0)),
            pl.BlockSpec((1, width // w_blocks, ff), lambda i: (i // w_blocks, i % w_blocks, 0)),
            pl.BlockSpec((1, ff // w_blocks, width), lambda i: (i // w_blocks, i % w_blocks, 0)),
        ),
        name="finish",
    )(tokens, grad_out, so, wr, st, x, g, hid, pg)

    out_rows = width // (seq_n * exp_n)
    n_scatter = seq_n * half
    pack = max(1, 128 // slots)
    tile = (out_rows // pack, slots * pack)
    grad_router = pl.pallas_call(
        functools.partial(scatter, seq_n, exp_n),
        out_shape=shape((out_rows, slots), F32),
        in_specs=[vmem],
        out_specs=vmem,
        scratch_shapes=[
            pltpu.VMEM((2, seq_n, half) + tile, BF16),
            pltpu.VMEM((seq_n, half) + tile, BF16),
            pltpu.VMEM((seq_n, half) + tile, BF16),
            pltpu.VMEM((seq_n * half - 1,) + tile, BF16),
            pltpu.SemaphoreType.DMA((n_scatter,)),
            pltpu.SemaphoreType.DMA((n_scatter,)),
        ],
        compiler_params=pltpu.CompilerParams(collective_id=1, has_side_effects=True),
        name="scatter",
    )(gr)
    return mixed, grad_tokens, grad_router, grad_w_in, grad_w_out


def solution(mesh):
    return jax.shard_map(
        functools.partial(on_device, mesh.shape["seq"], mesh.shape["exp"]),
        mesh=mesh,
        in_specs=(
            P(None, ("seq", "exp"), None),
            P(),
            P("exp", None, "seq"),
            P("exp", "seq", None),
            P(None, ("seq", "exp"), None),
        ),
        out_specs=(
            P(None, ("seq", "exp"), None),
            P(None, ("seq", "exp"), None),
            P(("seq", "exp"), None),
            P("exp", None, "seq"),
            P("exp", "seq", None),
        ),
        check_vma=False,
    )
```

profile of v0, /device:TPU:0, one launch (start us, length us, event | category | flops | bytes accessed | tf_op | source)
XLA Modules:
  0.0 65.6 jit_solution(12035692796979803852)
XLA Ops:
  0.6 40.8 %front.1 = (bf16[2,64,1024]{2,1,0:T(8,128)(2,1)}, bf16[2,128,1024]{2,1,0:T(8,128)(2,1)}, f32[8,64]{1,0:T(8,128)}, f32[2,16,1024]{2,1,0:T(8,128)}, bf16[16,1024]{...) custom-call(bf16[2,768,1024]{2,1,0:T(8,128)(2,1)} %tok.1, bf16[64,1024]{1,0:T(8,128)(2,1)} %bitcast.1, ...), custom_call_target="tpu_custom_call" | custom-call | tf_op jit(solution)/shard_map/front/pallas_call | solution.py:463
  41.5 12.2 %finish.1 = (bf16[2,768,1024]{2,1,0:T(8,128)(2,1)}, bf16[2,768,1024]{2,1,0:T(8,128)(2,1)}, f32[64,1024]{1,0:T(8,128)}, bf16[2,1024,1024]{2,1,0:T(8,128)(2,1)}, bf16[2,1024,1024]{2,1,0:T(8,128)(2,1)}) custom-call(bf16[2,768,1024]{2,1,0:T(8,128)(2,1)} %tok.1, bf16[2,768,1024]{2,1,0:T(8,128)(2,1)} %gout.1, bf16[2,64,1024]{2,1,0:T(8,128)(2,1)} %get-tuple-element.17.so, ...), custom_call_target="tpu_custom_call" | custom-call | tf_op jit(solution)/shard_map/finish/pallas_call | solution.py:523
  53.7 10.5 %scatter.1 = f32[32,64]{1,0:T(8,128)} custom-call(f32[64,1024]{1,0:T(8,128)} %get-tuple-element.26.gr), custom_call_target="tpu_custom_call" | custom-call | tf_op jit(solution)/shard_map/scatter/pallas_call | solution.py:558
  64.2 1.3 %copy.11 = f32[32,64]{1,0:T(8,128)} copy(f32[32,64]{1,0:T(8,128)} %scatter.1) | data formatting | bytes 16384
where the time goes:
time: 65.8 us; the launch traced here: 65.6 us
  Pallas kernels  63.6 us (97%)
  local copies, waits for them, and re-layouts  1.32 us (2%)
    pallas_call x1, Pallas kernels, on_device(): pl.pallas_call(functools.partial(front, seq_n, exp_n), out_shape=(shape((...  40.8 us
    pallas_call x1, Pallas kernels, on_device(): pl.pallas_call(functools.partial(finish, clips, steps), grid=(steps,), ou...  12.2 us
    pallas_call x1, Pallas kernels, on_device(): pl.pallas_call(functools.partial(scatter, seq_n, exp_n), out_shape=shape(...  10.5 us
    unnamed x1, local copies, waits for them, and re-layouts  1.32 us

commit v1 on v0

v1 whole, which is shorter than its diff:
```python
import functools

import jax
import jax.numpy as jnp
from jax import lax
from jax.experimental import pallas as pl
from jax.experimental.pallas import tpu as pltpu
from jax.sharding import PartitionSpec as P

MESH = pl.DeviceIdType.MESH
F32 = jnp.float32
BF16 = jnp.bfloat16
NT = (((1,), (1,)), ((), ()))
VMEM_BYTES = 67043328


def dot(a, b):
    return jnp.dot(a, b, preferred_element_type=F32)


def dot_nt(a, b):
    return lax.dot_general(a, b, NT, preferred_element_type=F32)


def place(seq_n, exp_n):
    s = lax.axis_index("seq")
    e = lax.axis_index("exp")
    half = exp_n // 2
    h, par = e // 2, e % 2
    pair = (s, h * 2 + (1 - par))
    seq_peers = [((s + k) % seq_n, e) for k in range(1, seq_n)]
    exp_peers = [(s, ((h + k) % half) * 2 + par) for k in range(1, half)]
    there = [((s + a) % seq_n, (h + b) % half) for a in range(seq_n) for b in range(half) if a or b]
    return s, h, par, pair, seq_peers, exp_peers, there


class Sender:
    def __init__(self, send_sem, recv_sem):
        self.send_sem, self.recv_sem, self.count, self.open = send_sem, recv_sem, 0, []

    def start(self, src, dst, peer):
        copy = pltpu.make_async_remote_copy(
            src_ref=src,
            dst_ref=dst,
            send_sem=self.send_sem.at[self.count],
            recv_sem=self.recv_sem.at[self.count],
            device_id=peer,
            device_id_type=MESH,
        )
        copy.start()
        self.count += 1
        self.open.append(copy)
        return copy

    def drain(self):
        for copy in self.open:
            copy.wait_send()


def copies_of(seq_n, exp_n):
    half = exp_n // 2
    reduce = 3 + 3 * (half - 1) + 3 * (seq_n - 1)
    gather = 2 * (seq_n - 1) + 4 * (half - 1) + 4 * half
    return reduce + gather + seq_n * half


def arrived(copies):
    for copy in copies:
        copy.wait_recv()


def stat_tile(*columns):
    shape = columns[0].shape[:-1] + (128,)
    lane = lax.broadcasted_iota(jnp.int32, shape, len(shape) - 1)
    tile = jnp.zeros(shape, F32)
    for i, column in enumerate(columns):
        tile = jnp.where(lane == i, column, tile)
    return tile


def join(parts):
    peak = parts[0][0]
    for p, _ in parts[1:]:
        peak = jnp.maximum(peak, p)
    factors = [jnp.exp(p - peak) for p, _ in parts]
    mass = factors[0] * parts[0][1]
    for f, (_, m) in zip(factors[1:], parts[1:]):
        mass = mass + f * m
    return peak, mass, factors


def split_stats(tile):
    return tile[..., 0:1], tile[..., 1:2]


def layer(
    seq_n, exp_n, tok_hbm, rt_hbm, gout_hbm, win_hbm, wout_hbm,
    mixed, gt, gwin, gwout, gr_o,
    tok, gout, rt, win, wout, lg, qf, dsp, lm, xt, qt,
    buf_a, rcv_a, buf_b, rcv_b, xg, se, ag,
    st_a, st_p, st_b, st_z, st_c, sa,
    gr_a, gr_p, gr_b, gr_r,
    w_sem, send_sem, recv_sem,
):
    clips, rows, width = tok.shape
    slots = rt.shape[0]
    half = exp_n // 2
    owned = slots // exp_n
    nr = clips * owned
    experts = win.shape[0]
    s, h, par, pair, seq_peers, exp_peers, there = place(seq_n, exp_n)
    far_peers = [(t, g * 2 + par) for t, g in there]

    load_rt = pltpu.make_async_copy(rt_hbm, rt, w_sem.at[0])
    load_tok = [pltpu.make_async_copy(tok_hbm.at[c], tok.at[c], w_sem.at[1 + c]) for c in range(clips)]
    load_gout = [
        pltpu.make_async_copy(gout_hbm.at[c], gout.at[c], w_sem.at[1 + clips + c]) for c in range(clips)
    ]
    load_in = pltpu.make_async_copy(win_hbm, win, w_sem.at[1 + 2 * clips])
    load_out = pltpu.make_async_copy(wout_hbm, wout, w_sem.at[2 + 2 * clips])
    load_rt.start()
    for load in load_tok:
        load.start()
    barrier = pltpu.get_barrier_semaphore()
    for peer in [pair] + far_peers:
        pl.semaphore_signal(barrier, inc=1, device_id=peer, device_id_type=MESH)
    net = Sender(send_sem, recv_sem)

    load_rt.wait()
    peaks, masses = [], []
    for c in range(clips):
        load_tok[c].wait()
        load_gout[c].start()
        value = dot_nt(rt[...], tok[c])
        lg[c] = value
        peak = jnp.max(value, axis=1, keepdims=True)
        p = jnp.exp(value - peak)
        peaks.append(peak.reshape(exp_n, owned, 1))
        masses.append(jnp.sum(p, axis=1, keepdims=True).reshape(exp_n, owned, 1))
        xt[c] = p.astype(BF16)
        q = jnp.exp(value - jnp.max(value, axis=0, keepdims=True))
        q = q / jnp.sum(q, axis=0, keepdims=True)
        qf[c] = q
        qt[c] = q.astype(BF16)
    load_out.start()
    load_in.start()
    tile = stat_tile(jnp.concatenate(peaks, axis=1), jnp.concatenate(masses, axis=1))
    tile = tile.reshape(half, 2, nr, 128)
    for q in range(2):
        st_a[q] = tile[:, q]

    def lay_out(kind, values):
        for g in range(half):
            for q in range(2):
                at = (2 * g + q) * owned
                rows_ = [value[at : at + owned] for value in values]
                buf_a[kind, q, g] = jnp.concatenate(rows_, axis=0).astype(BF16)

    def to_pair(kind):
        return [net.start(buf_a.at[kind, 1 - par], rcv_a.at[kind], pair)]

    def to_exp(kind, factors=None):
        for g in range(half):
            mine = buf_a[kind, par, g].astype(F32)
            other = rcv_a[kind, g].astype(F32)
            if factors is not None:
                mine, other = mine * factors[0][g], other * factors[1][g]
            buf_b[kind, g] = (mine + other).astype(BF16)
        return [
            net.start(buf_b.at[kind, (h + 1 + k) % half], rcv_b.at[kind, k], peer)
            for k, peer in enumerate(exp_peers)
        ]

    def to_seq(kind, factors=None):
        parts = [buf_b[kind, h].astype(F32)] + [rcv_b[kind, k].astype(F32) for k in range(half - 1)]
        if factors is not None:
            parts = [part * f for part, f in zip(parts, factors)]
        total = parts[0]
        for part in parts[1:]:
            total = total + part
        xg[kind, s] = total.astype(BF16)
        return [net.start(xg.at[kind, s], xg.at[kind, s], peer) for peer in seq_peers]

    def seq_total(ref, kind, factors=None):
        total = None
        for t in range(seq_n):
            part = ref[kind, t].astype(F32)
            if factors is not None:
                part = part * factors[t]
            total = part if total is None else total + part
        return total

    pl.semaphore_wait(barrier, 1 + len(far_peers))
    stat = [net.start(st_a.at[1 - par], st_p, pair)]
    lay_out(0, [dot(xt[c], tok[c]) for c in range(clips)])
    inputs = to_pair(0)
    for load in load_gout:
        load.wait()
    lay_out(1, [dot(qt[c], gout[c]) for c in range(clips)])
    grads = to_pair(1)
    arrived(stat)
    peak, mass, fac = join([split_stats(st_a[par]), split_stats(st_p[...])])
    st_b[...] = stat_tile(peak, mass)
    stat = [net.start(st_b.at[(h + 1 + k) % half], st_z.at[k], peer) for k, peer in enumerate(exp_peers)]
    arrived(inputs)
    inputs = to_exp(0, fac)
    arrived(grads)
    grads = to_exp(1)
    arrived(stat)
    peak, mass, fac = join([split_stats(st_b[h])] + [split_stats(st_z[k]) for k in range(half - 1)])
    st_c[s] = stat_tile(peak, mass)
    stat = [net.start(st_c.at[s], st_c.at[s], peer) for peer in seq_peers]
    arrived(inputs)
    inputs = to_seq(0, fac)
    arrived(grads)
    grads = to_seq(1)
    arrived(stat)
    peak, mass, fac = join([split_stats(st_c[t]) for t in range(seq_n)])
    fac = [f / mass for f in fac]
    sa[0, h, par] = stat_tile(peak, mass)

    row = lax.broadcasted_iota(jnp.int32, (nr, 1), 0)
    expert_of = (row % owned) // (owned // experts)
    mask = [(expert_of == e).astype(F32) for e in range(experts)]
    load_out.wait()
    load_in.wait()
    arrived(inputs)
    x_rows = seq_total(xg, 0, fac)
    pre = 0.0
    for e in range(experts):
        pre = pre + dot((x_rows * mask[e]).astype(BF16), win[e])
    hidden, back = jax.vjp(jax.nn.gelu, pre)

    def share(kind, part):
        se[kind, s] = part.astype(BF16)
        return [net.start(se.at[kind, s], se.at[kind, s], peer) for peer in seq_peers]

    out_part = 0.0
    for e in range(experts):
        out_part = out_part + dot((hidden * mask[e]).astype(BF16), wout[e])
    forward = share(0, out_part)
    arrived(grads)
    g_rows = seq_total(xg, 1).astype(BF16)
    hidden_grad = 0.0
    for e in range(experts):
        hidden_grad = hidden_grad + dot_nt(g_rows, wout[e]) * mask[e]
    pre_grad = back(hidden_grad)[0]
    in_part = 0.0
    for e in range(experts):
        in_part = in_part + dot_nt((pre_grad * mask[e]).astype(BF16), win[e])
    backward = share(1, in_part)

    def send_piece(kind, peers, g, q):
        copies = []
        for peer in peers:
            at, st = ag.at[kind, g, q], sa.at[kind, g, q]
            copies.append([net.start(st, st, peer), net.start(at, at, peer)])
        return copies

    def make_piece(kind):
        piece = seq_total(se, kind).astype(BF16)
        ag[kind, h, par] = piece
        if kind == 1:
            sa[1, h, par] = stat_tile(jnp.sum(piece.astype(F32) * x_rows, axis=1, keepdims=True))
        along = send_piece(kind, exp_peers, h, par)
        across = send_piece(kind, [pair], h, par)
        return along, across

    def pass_on(kind, along, across):
        for k in range(half - 1):
            arrived(along[k])
            across += send_piece(kind, [pair], (h + half - 1 - k) % half, par)

    def weight_grad(out, e, left, right):
        out[e] = dot((left * mask[e]).T.astype(BF16), right).astype(BF16)

    weight_grad(gwout, 0, hidden, g_rows)
    arrived(forward)
    along0, across0 = make_piece(0)
    for e in range(1, experts):
        weight_grad(gwout, e, hidden, g_rows)
    arrived(backward)
    along1, across1 = make_piece(1)
    pg = pre_grad.astype(BF16)
    for e in range(experts):
        weight_grad(gwin, e, x_rows, pg)
    pass_on(0, along0, across0)

    def of_clip(value, c):
        return value.reshape(exp_n, clips, owned, value.shape[-1])[:, c].reshape(slots, value.shape[-1])

    def spread(value, c):
        value = value.reshape(exp_n, 1, owned, value.shape[-1])
        zero = jnp.zeros_like(value)
        parts = [value if k == c else zero for k in range(clips)]
        return jnp.concatenate(parts, axis=1).reshape(clips * slots, value.shape[-1])

    for step in across0:
        arrived(step)
    so = ag[0].reshape(exp_n * nr, width)
    stats = sa[0].reshape(exp_n * nr, 128)
    for c in range(clips):
        mixing = qf[c]
        mixing_grad = of_clip(dot_nt(so, gout[c]), c)
        lm[c] = mixing * (mixing_grad - jnp.sum(mixing * mixing_grad, axis=0, keepdims=True))
        mine = of_clip(stats, c)
        dsp[c] = jnp.exp(lg[c] - mine[:, 0:1]) / mine[:, 1:2]
    pass_on(1, along1, across1)
    for c in range(clips):
        mixed[c] = dot(spread(qf[c], c).T.astype(BF16), so).astype(BF16)
    for step in across1:
        arrived(step)
    sig = ag[1].reshape(exp_n * nr, width)
    inner = sa[1].reshape(exp_n * nr, 128)
    gr = 0.0
    for c in range(clips):
        dispatch_grad = of_clip(dot_nt(sig, tok[c]), c)
        lgrad = dsp[c] * (dispatch_grad - of_clip(inner, c)[:, 0:1]) + lm[c]
        lm[c] = lgrad
        gr = gr + dot(lgrad.astype(BF16), tok[c])

    out_rows = gr_o.shape[0]
    packed = gr_b.shape[2]
    pack = out_rows // packed
    whole = gr.T
    for t in range(seq_n):
        for g in range(half):
            for q in range(2):
                at = (t * exp_n + 2 * g + q) * out_rows
                parts = [whole[at + j * packed : at + (j + 1) * packed] for j in range(pack)]
                gr_a[q, t, g] = jnp.concatenate(parts, axis=1).astype(BF16)
    last = [net.start(gr_a.at[1 - par], gr_p, pair)]
    both = jnp.concatenate([rt[...], sig], axis=0)

    def token_grad(c):
        left = jnp.concatenate([lm[c], spread(dsp[c], c)], axis=0)
        gt[c] = dot(left.T.astype(BF16), both).astype(BF16)

    arrived(last)
    gr_b[...] = (gr_a[par].astype(F32) + gr_p[...].astype(F32)).astype(BF16)
    last = [net.start(gr_b.at[t, g], gr_r.at[k], far_peers[k]) for k, (t, g) in enumerate(there)]
    for c in range(clips):
        token_grad(c)
    total = gr_b[s, h].astype(F32)
    for k, copy in enumerate(last):
        copy.wait_recv()
        total = total + gr_r[k].astype(F32)
    for j in range(pack):
        gr_o[j * packed : (j + 1) * packed] = total[:, j * slots : (j + 1) * slots]
    net.drain()


def put_out(n, *refs):
    ins, outs, sem = refs[:n], refs[n : 2 * n], refs[2 * n]
    copies = []
    for src, dst in zip(ins, outs):
        copies.append(pltpu.make_async_copy(src, dst, sem.at[len(copies)]))
        copies[-1].start()
    for copy in copies:
        copy.wait()


def on_device(seq_n, exp_n, tokens, router, w_in, w_out, grad_out):
    clips, rows, width = tokens.shape
    slots = router.shape[1]
    half = exp_n // 2
    owned = slots // exp_n
    nr = clips * owned
    vmem = pl.BlockSpec(memory_space=pltpu.VMEM)
    hbm = pl.BlockSpec(memory_space=pltpu.HBM)
    anywhere = pl.BlockSpec(memory_space=pl.ANY)
    shape = jax.ShapeDtypeStruct
    out_rows = width // (seq_n * exp_n)
    pack = max(1, 128 // slots)
    tile = (out_rows // pack, slots * pack)
    piece = (nr, width)
    stat = (nr, 128)
    n_copies = copies_of(seq_n, exp_n)
    outs = (
        shape(tokens.shape, BF16),
        shape(tokens.shape, BF16),
        shape(w_in.shape, BF16),
        shape(w_out.shape, BF16),
        shape((out_rows, slots), F32),
    )
    out_bytes = sum(o.size * o.dtype.itemsize for o in outs)
    limit = 30 * 2**20
    results = pl.pallas_call(
        functools.partial(layer, seq_n, exp_n),
        out_shape=outs,
        in_specs=[hbm] * 5,
        out_specs=(vmem,) * 5,
        scratch_shapes=[
            pltpu.VMEM(tokens.shape, BF16),
            pltpu.VMEM(tokens.shape, BF16),
            pltpu.VMEM((slots, width), BF16),
            pltpu.VMEM(w_in.shape, BF16),
            pltpu.VMEM(w_out.shape, BF16),
            pltpu.VMEM((clips, slots, rows), F32),
            pltpu.VMEM((clips, slots, rows), F32),
            pltpu.VMEM((clips, slots, rows), F32),
            pltpu.VMEM((clips, slots, rows), F32),
            pltpu.VMEM((clips, slots, rows), BF16),
            pltpu.VMEM((clips, slots, rows), BF16),
            pltpu.VMEM((2, 2, half) + piece, BF16),
            pltpu.VMEM((2, half) + piece, BF16),
            pltpu.VMEM((2, half) + piece, BF16),
            pltpu.VMEM((2, half - 1) + piece, BF16),
            pltpu.VMEM((2, seq_n) + piece, BF16),
            pltpu.VMEM((2, seq_n) + piece, BF16),
            pltpu.VMEM((2, half, 2) + piece, BF16),
            pltpu.VMEM((2, half) + stat, F32),
            pltpu.VMEM((half,) + stat, F32),
            pltpu.VMEM((half,) + stat, F32),
            pltpu.VMEM((half - 1,) + stat, F32),
            pltpu.VMEM((seq_n,) + stat, F32),
            pltpu.VMEM((2, half, 2) + stat, F32),
            pltpu.VMEM((2, seq_n, half) + tile, BF16),
            pltpu.VMEM((seq_n, half) + tile, BF16),
            pltpu.VMEM((seq_n, half) + tile, BF16),
            pltpu.VMEM((seq_n * half - 1,) + tile, BF16),
            pltpu.SemaphoreType.DMA((2 * clips + 3,)),
            pltpu.SemaphoreType.DMA((n_copies,)),
            pltpu.SemaphoreType.DMA((n_copies,)),
        ],
        compiler_params=pltpu.CompilerParams(
            collective_id=0, has_side_effects=True, vmem_limit_bytes=limit
        ),
        name="layer",
    )(tokens, router.T, grad_out, w_in, w_out)
    mixed, grad_tokens, grad_w_in, grad_w_out, grad_router = pl.pallas_call(
        functools.partial(put_out, len(outs)),
        out_shape=outs,
        in_specs=[anywhere] * len(outs),
        out_specs=(hbm,) * len(outs),
        scratch_shapes=[pltpu.SemaphoreType.DMA((len(outs),))],
        compiler_params=pltpu.CompilerParams(vmem_limit_bytes=2**20),
        name="put_out",
    )(*results)
    return mixed, grad_tokens, grad_router, grad_w_in, grad_w_out


def solution(mesh):
    return jax.shard_map(
        functools.partial(on_device, mesh.shape["seq"], mesh.shape["exp"]),
        mesh=mesh,
        in_specs=(
            P(None, ("seq", "exp"), None),
            P(),
            P("exp", None, "seq"),
            P("exp", "seq", None),
            P(None, ("seq", "exp"), None),
        ),
        out_specs=(
            P(None, ("seq", "exp"), None),
            P(None, ("seq", "exp"), None),
            P(("seq", "exp"), None),
            P("exp", None, "seq"),
            P("exp", "seq", None),
        ),
        check_vma=False,
    )
```

time: 65.8 us -> 53.9 us (0.82)
  Pallas kernels: 63.6 us -> 48.4 us
  local copies, waits for them, and re-layouts: 1.32 us -> 4.68 us
    pallas_call x3 -> x2, Pallas kernels: 63.6 us -> 48.4 us  [the longest x1 43 us: on_device(): pl.pallas_call(functools.partial(layer, seq_n, exp_n), out_shape=outs, in...]
    unnamed x1 -> x6, local copies, waits for them, and re-layouts: 1.32 us -> 4.68 us
where the time goes in v1:
time: 53.9 us; the launch traced here: 53.7 us
  Pallas kernels  48.4 us (90%)
  local copies, waits for them, and re-layouts  4.68 us (9%)
  between operations  0.65 us (1%)
    pallas_call x1, Pallas kernels, on_device(): pl.pallas_call(functools.partial(layer, seq_n, exp_n), out_shape=outs, in...  43 us
    pallas_call x1, Pallas kernels, on_device(): pl.pallas_call(functools.partial(put_out, len(outs)), out_shape=outs, in_...  5.39 us
    unnamed x6, local copies, waits for them, and re-layouts  4.68 us

profile of v1, /device:TPU:0, one launch (start us, length us, event | category | flops | bytes accessed | tf_op | source)
XLA Modules:
  0.0 53.7 jit_solution(3704598517779107971)
XLA Ops:
  0.6 0.0 copy-start
  0.6 1.9 %copy-done = bf16[2,768,1024]{2,1,0:T(8,128)(2,1)S(1)} copy-done((bf16[2,768,1024]{2,1,0:T(8,128)(2,1)S(1)}, bf16[2,768,1024]{2,1,0:T(8,128)(2,1)}, u32[]{:S(2)}) %copy-start) | copy-done | bytes 3145752
  2.5 0.0 copy-start.1
  2.5 1.9 %copy-done.1 = bf16[2,768,1024]{2,1,0:T(8,128)(2,1)S(1)} copy-done((bf16[2,768,1024]{2,1,0:T(8,128)(2,1)S(1)}, bf16[2,768,1024]{2,1,0:T(8,128)(2,1)}, u32[]{:S(2)}) %copy-start.1) | copy-done | bytes 3145752
  4.4 0.0 copy-start.2
  4.4 0.9 %copy-done.2 = bf16[1024,64]{0,1:T(8,128)(2,1)S(1)} copy-done((bf16[1024,64]{0,1:T(8,128)(2,1)S(1)}, bf16[1024,64]{0,1:T(8,128)(2,1)}, u32[]{:S(2)}) %copy-start.2) | copy-done | bytes 131096
  5.3 43.0 %layer.1 = (bf16[2,768,1024]{2,1,0:T(8,128)(2,1)S(1)}, bf16[2,768,1024]{2,1,0:T(8,128)(2,1)S(1)}, bf16[2,1024,1024]{2,1,0:T(8,128)(2,1)S(1)}, bf16[2,1024,1024]{2,1,0:T(8,128)(2,1)S(1)}, f32[32,64]{1,0:T(8,128)S(1)}) custom-call(bf16[2,768,1024]{2,1,0:T(8,128)(2,1)S(1)} %copy-done, bf16[64,1024]{1,0:T(8,128)(2,1)S(1)} %bitcast.1, ...), custom_call_target="tpu_custom_call" | custom-call | tf_op jit(solution)/shard_map/layer/pallas_call | solution.py:388
  48.3 5.4 %put_out.1 = (bf16[2,768,1024]{2,1,0:T(8,128)(2,1)}, bf16[2,768,1024]{2,1,0:T(8,128)(2,1)}, bf16[2,1024,1024]{2,1,0:T(8,128)(2,1)}, bf16[2,1024,1024]{2,1,0:T(8,128)(2,1)}, f32[32,64]{1,0:T(8,128)}) custom-call(bf16[2,768,1024]{2,1,0:T(8,128)(2,1)S(1)} %get-tuple-element.15.refs_0_, bf16[2,768,1024]{2,1,0:T(8,128)(2,1)S(1)} %get-tuple-element.16.refs_1_, ...), custom_call_target="tpu_custom_call" | custom-call | tf_op jit(solution)/shard_map/put_out/pallas_call | solution.py:431
Async XLA Ops:
  0.6 1.9 %copy-start = (bf16[2,768,1024]{2,1,0:T(8,128)(2,1)S(1)}, bf16[2,768,1024]{2,1,0:T(8,128)(2,1)}, u32[]{:S(2)}) copy-start(bf16[2,768,1024]{2,1,0:T(8,128)(2,1)} %tok_hbm.1) | copy-start | bytes 9437188
  2.5 1.9 %copy-start.1 = (bf16[2,768,1024]{2,1,0:T(8,128)(2,1)S(1)}, bf16[2,768,1024]{2,1,0:T(8,128)(2,1)}, u32[]{:S(2)}) copy-start(bf16[2,768,1024]{2,1,0:T(8,128)(2,1)} %gout_hbm.1) | copy-start | bytes 9437188
  4.4 0.9 %copy-start.2 = (bf16[1024,64]{0,1:T(8,128)(2,1)S(1)}, bf16[1024,64]{0,1:T(8,128)(2,1)}, u32[]{:S(2)}) copy-start(bf16[1024,64]{0,1:T(8,128)(2,1)} %param.6) | copy-start | bytes 393220

commit v2 on v1

--- a/solution.py
+++ b/solution.py
@@ -383,8 +383,7 @@
         shape(w_out.shape, BF16),
         shape((out_rows, slots), F32),
     )
-    out_bytes = sum(o.size * o.dtype.itemsize for o in outs)
-    limit = 30 * 2**20
+    limit = VMEM_BYTES // 2
     results = pl.pallas_call(
         functools.partial(layer, seq_n, exp_n),
         out_shape=outs,
@@ -427,7 +426,7 @@
             collective_id=0, has_side_effects=True, vmem_limit_bytes=limit
         ),
         name="layer",
-    )(tokens, router.T, grad_out, w_in, w_out)
+    )(*[pltpu.with_memory_space_constraint(a, pltpu.HBM) for a in (tokens, router.T, grad_out, w_in, w_out)])
     mixed, grad_tokens, grad_w_in, grad_w_out, grad_router = pl.pallas_call(
         functools.partial(put_out, len(outs)),
         out_shape=outs,

time: 53.9 us -> 49.2 us (0.913)
  local copies, waits for them, and re-layouts: 4.68 us -> 0 us
    unnamed x6 -> x0, local copies, waits for them, and re-layouts: 4.68 us -> none
where the time goes in v2:
time: 49.2 us; the launch traced here: 49.1 us
  Pallas kernels  48.4 us (98%)
  between operations  0.64 us (1%)
    pallas_call x1, Pallas kernels, on_device(): pl.pallas_call(functools.partial(layer, seq_n, exp_n), out_shape=outs, in...  43 us
    pallas_call x1, Pallas kernels, on_device(): pl.pallas_call(functools.partial(put_out, len(outs)), out_shape=outs, in_...  5.39 us

profile of v2, /device:TPU:0, one launch (start us, length us, event | category | flops | bytes accessed | tf_op | source)
XLA Modules:
  0.0 49.1 jit_solution(562108438420575313)
XLA Ops:
  0.6 43.0 %layer.1 = (bf16[2,768,1024]{2,1,0:T(8,128)(2,1)S(1)}, bf16[2,768,1024]{2,1,0:T(8,128)(2,1)S(1)}, bf16[2,1024,1024]{2,1,0:T(8,128)(2,1)S(1)}, bf16[2,1024,1024]{2,1,0:T(8,128)(2,1)S(1)}, f32[32,64]{1,0:T(8,128)S(1)}) custom-call(bf16[2,768,1024]{2,1,0:T(8,128)(2,1)} %tok_hbm.1, bf16[64,1024]{1,0:T(8,128)(2,1)} %bitcast.1, bf16[2,768,1024]{2,1,0:T(8,128)(2,1)} %gout_hbm.1, ...), custom_call_target="tpu_custom_call" | custom-call | tf_op jit(solution)/shard_map/layer/pallas_call | solution.py:387
  43.7 5.4 %put_out.1 = (bf16[2,768,1024]{2,1,0:T(8,128)(2,1)}, bf16[2,768,1024]{2,1,0:T(8,128)(2,1)}, bf16[2,1024,1024]{2,1,0:T(8,128)(2,1)}, bf16[2,1024,1024]{2,1,0:T(8,128)(2,1)}, f32[32,64]{1,0:T(8,128)}) custom-call(bf16[2,768,1024]{2,1,0:T(8,128)(2,1)S(1)} %get-tuple-element.15.refs_0_, bf16[2,768,1024]{2,1,0:T(8,128)(2,1)S(1)} %get-tuple-element.16.refs_1_, ...), custom_call_target="tpu_custom_call" | custom-call | tf_op jit(solution)/shard_map/put_out/pallas_call | solution.py:430

commit v3 on v2

v3 whole, which is shorter than its diff:
```python
import functools

import jax
import jax.numpy as jnp
from jax import lax
from jax.experimental import pallas as pl
from jax.experimental.pallas import tpu as pltpu
from jax.sharding import PartitionSpec as P

MESH = pl.DeviceIdType.MESH
F32 = jnp.float32
BF16 = jnp.bfloat16
NT = (((1,), (1,)), ((), ()))
VMEM_BYTES = 67043328


def dot(a, b):
    return jnp.dot(a, b, preferred_element_type=F32)


def dot_nt(a, b):
    return lax.dot_general(a, b, NT, preferred_element_type=F32)


def place(seq_n, exp_n):
    s = lax.axis_index("seq")
    e = lax.axis_index("exp")
    half = exp_n // 2
    h, par = e // 2, e % 2
    pair = (s, h * 2 + (1 - par))
    seq_peers = [((s + k) % seq_n, e) for k in range(1, seq_n)]
    exp_peers = [(s, ((h + k) % half) * 2 + par) for k in range(1, half)]
    there = [((s + a) % seq_n, (h + b) % half) for a in range(seq_n) for b in range(half) if a or b]
    return s, h, par, pair, seq_peers, exp_peers, there


class Net:
    def __init__(self, send_sem, recv_sem):
        self.send_sem, self.recv_sem, self.groups = send_sem, recv_sem, []

    def group(self, whole):
        self.groups.append(whole)
        return Group(self, len(self.groups) - 1, whole)

    def drain(self):
        for i, whole in enumerate(self.groups):
            pltpu.make_async_copy(whole, whole, self.send_sem.at[i]).wait()


class Group:
    def __init__(self, net, index, whole):
        self.net, self.index, self.whole = net, index, whole

    def start(self, src, dst, peer):
        pltpu.make_async_remote_copy(
            src_ref=src,
            dst_ref=dst,
            send_sem=self.net.send_sem.at[self.index],
            recv_sem=self.net.recv_sem.at[self.index],
            device_id=peer,
            device_id_type=MESH,
        ).start()
        return self

    def show(self, peers, ref, *at):
        for peer in peers:
            self.start(ref.at[at], ref.at[at], peer)
        return self

    def arrived(self):
        pltpu.make_async_copy(self.whole, self.whole, self.net.recv_sem.at[self.index]).wait()


def groups_of(seq_n, exp_n):
    return 21 + (seq_n - 1) + (exp_n // 2 - 1)


def stat_tile(columns):
    shape = columns[0].shape[:-1] + (128,)
    lane = lax.broadcasted_iota(jnp.int32, shape, len(shape) - 1)
    tile = jnp.zeros(shape, F32)
    for i, column in enumerate(columns):
        tile = jnp.where(lane == i, column, tile)
    return tile


def by_clip(column, clips):
    owned = column.shape[-2] // clips
    return [column[..., c * owned : (c + 1) * owned, :] for c in range(clips)]


def split_stats(tile, clips):
    lanes = [tile[..., i : i + 1] for i in range(2 * clips)]
    axis = len(tile.shape) - 2
    return jnp.concatenate(lanes[:clips], axis=axis), jnp.concatenate(lanes[clips:], axis=axis)


def join(parts):
    peak = parts[0][0]
    for p, _ in parts[1:]:
        peak = jnp.maximum(peak, p)
    factors = [jnp.exp(p - peak) for p, _ in parts]
    mass = factors[0] * parts[0][1]
    for f, (_, m) in zip(factors[1:], parts[1:]):
        mass = mass + f * m
    return peak, mass, factors


def layer(
    seq_n, exp_n, tok_hbm, rt_hbm, gout_hbm, win_hbm, wout_hbm,
    mixed, gt, gwin, gwout, gr_o,
    tok, gout, rt, win, wout, lg, qf, dsp, lm, xt, qt,
    buf_a, rcv_a, xb, xr, xg, gb, gbr, gc, gcr, gg, fe, fer, se, so_ag, sig_ag,
    st_a, st_p, st_b, st_z, st_c, sa, si,
    gr_a, gr_p, gr_b, gr_r,
    w_sem, send_sem, recv_sem,
):
    clips, rows, width = tok.shape
    slots = rt.shape[0]
    half = exp_n // 2
    owned = slots // exp_n
    nr = clips * owned
    dc = width // seq_n
    experts = win.shape[0]
    s, h, par, pair, seq_peers, exp_peers, there = place(seq_n, exp_n)
    far_peers = [(t, g * 2 + par) for t, g in there]

    load_rt = pltpu.make_async_copy(rt_hbm, rt, w_sem.at[0])
    load_tok = [pltpu.make_async_copy(tok_hbm.at[c], tok.at[c], w_sem.at[1 + c]) for c in range(clips)]
    load_gout = [
        pltpu.make_async_copy(gout_hbm.at[c], gout.at[c], w_sem.at[1 + clips + c]) for c in range(clips)
    ]
    load_in = pltpu.make_async_copy(win_hbm, win, w_sem.at[1 + 2 * clips])
    load_out = pltpu.make_async_copy(wout_hbm, wout, w_sem.at[2 + 2 * clips])
    load_rt.start()
    for load in load_tok:
        load.start()
    barrier = pltpu.get_barrier_semaphore()
    for peer in [pair] + far_peers:
        pl.semaphore_signal(barrier, inc=1, device_id=peer, device_id_type=MESH)
    net = Net(send_sem, recv_sem)

    load_rt.wait()
    values, peaks, masses = [], [], []
    for c in range(clips):
        load_tok[c].wait()
        load_gout[c].start()
        values.append(dot_nt(rt[...], tok[c]))
    for c, value in enumerate(values):
        lg[c] = value
        peak = jnp.max(value, axis=1, keepdims=True)
        p = jnp.exp(value - peak)
        peaks.append(peak.reshape(half, 2, owned, 1))
        masses.append(jnp.sum(p, axis=1, keepdims=True).reshape(half, 2, owned, 1))
        xt[c] = p.astype(BF16)
    for c, value in enumerate(values):
        q = jnp.exp(value - jnp.max(value, axis=0, keepdims=True))
        q = q / jnp.sum(q, axis=0, keepdims=True)
        qf[c] = q
        qt[c] = q.astype(BF16)
    tile = stat_tile(peaks + masses)
    for q in range(2):
        st_a[q] = tile[:, q]

    def lay_out(kind, values):
        for g in range(half):
            for q in range(2):
                at = (2 * g + q) * owned
                rows_ = [value[at : at + owned] for value in values]
                buf_a[kind, q, g] = jnp.concatenate(rows_, axis=0).astype(BF16)

    def pair_sum(kind, g, factors=None):
        mine = buf_a[kind, par, g].astype(F32)
        other = rcv_a[kind, g].astype(F32)
        if factors is not None:
            mine, other = mine * factors[0][g], other * factors[1][g]
        return (mine + other).astype(BF16)

    def spread_over(peers, at, ref, dst):
        group = net.group(dst)
        for k, peer in enumerate(peers):
            group.start(ref.at[at(k)], dst.at[k], peer)
        return group

    def show_seq(ref):
        return net.group(ref.at[pl.ds(0, seq_n - 1)]).show(seq_peers, ref, s)

    def exp_of(k):
        return (h + 1 + k) % half

    def seq_of(k):
        return (s + 1 + k) % seq_n

    def add_up(parts, factors=None):
        parts = [part.astype(F32) for part in parts]
        if factors is not None:
            parts = [part * f for part, f in zip(parts, factors)]
        total = parts[0]
        for part in parts[1:]:
            total = total + part
        return total

    lay_out(0, [dot(xt[c], tok[c]) for c in range(clips)])
    pl.semaphore_wait(barrier, 1 + len(far_peers))
    stat = net.group(st_p).start(st_a.at[1 - par], st_p, pair)
    inputs = net.group(rcv_a.at[0]).start(buf_a.at[0, 1 - par], rcv_a.at[0], pair)
    for load in load_gout:
        load.wait()
    lay_out(1, [dot(qt[c], gout[c]) for c in range(clips)])
    grads = net.group(rcv_a.at[1]).start(buf_a.at[1, 1 - par], rcv_a.at[1], pair)
    load_out.start()
    load_in.start()

    stat.arrived()
    peak, mass, fac = join([split_stats(st_a[par], clips), split_stats(st_p[...], clips)])
    st_b[...] = stat_tile(by_clip(peak, clips) + by_clip(mass, clips))
    stat = spread_over(exp_peers, exp_of, st_b, st_z)
    inputs.arrived()
    for g in range(half):
        xb[g] = pair_sum(0, g, fac)
    inputs = spread_over(exp_peers, exp_of, xb, xr)
    grads.arrived()
    for g in range(half):
        value = pair_sum(1, g)
        for t in range(seq_n):
            gb[t, g] = value[:, t * dc : (t + 1) * dc]
    grads = spread_over(seq_peers, seq_of, gb, gbr)
    stat.arrived()
    parts = [split_stats(st_b[h], clips)] + [split_stats(st_z[k], clips) for k in range(half - 1)]
    peak, mass, fac = join(parts)
    st_c[s] = stat_tile(by_clip(peak, clips) + by_clip(mass, clips))
    stat = show_seq(st_c)
    grads.arrived()
    for g in range(half):
        gc[g] = add_up([gb[s, g]] + [gbr[k, g] for k in range(seq_n - 1)]).astype(BF16)
    grads = spread_over(exp_peers, exp_of, gc, gcr)
    inputs.arrived()
    xg[s] = add_up([xb[h]] + [xr[k] for k in range(half - 1)], fac).astype(BF16)
    inputs = show_seq(xg)
    stat.arrived()
    peak, mass, fac = join([split_stats(st_c[t], clips) for t in range(seq_n)])
    fac = [f / mass for f in fac]
    sa[h, par] = stat_tile(by_clip(peak, clips) + by_clip(mass, clips))
    stat_along = net.group(sa.at[pl.ds(0, half - 1), 0]).show(exp_peers, sa, h, par)
    stat_across = net.group(sa.at[pl.ds(0, half), 0]).show([pair], sa, h, par)
    grads.arrived()
    gg[s] = add_up([gc[h]] + [gcr[k] for k in range(half - 1)]).astype(BF16)
    grads = show_seq(gg)

    row = lax.broadcasted_iota(jnp.int32, (nr, 1), 0)
    expert_of = (row % owned) // (owned // experts)
    mask = [(expert_of == e).astype(F32) for e in range(experts)]
    load_out.wait()
    load_in.wait()
    inputs.arrived()
    x_rows = add_up([xg[t] for t in range(seq_n)], fac)
    pre = 0.0
    for e in range(experts):
        pre = pre + dot((x_rows * mask[e]).astype(BF16), win[e])
    hidden, back = jax.vjp(jax.nn.gelu, pre)
    out_part = 0.0
    for e in range(experts):
        out_part = out_part + dot((hidden * mask[e]).astype(BF16), wout[e])
    for t in range(seq_n):
        fe[t] = out_part[:, t * dc : (t + 1) * dc].astype(BF16)
    forward = spread_over(seq_peers, seq_of, fe, fer)
    grads.arrived()
    g_rows = jnp.concatenate([gg[t] for t in range(seq_n)], axis=1)
    hidden_grad = 0.0
    for e in range(experts):
        hidden_grad = hidden_grad + dot_nt(g_rows, wout[e]) * mask[e]
    pre_grad = back(hidden_grad)[0]
    in_part = 0.0
    for e in range(experts):
        in_part = in_part + dot_nt((pre_grad * mask[e]).astype(BF16), win[e])
    se[s] = in_part.astype(BF16)
    backward = show_seq(se)

    def from_exp(k):
        return (h + half - 1 - k) % half

    def weight_grad(out, e, left, right):
        out[e] = dot((left * mask[e]).T.astype(BF16), right).astype(BF16)

    forward.arrived()
    so_ag[par, s, h] = add_up([fe[s]] + [fer[k] for k in range(seq_n - 1)]).astype(BF16)
    forward = net.group(so_ag.at[0, 0, pl.ds(0, half - 1)]).show(exp_peers, so_ag, par, s, h)
    stat_along.arrived()
    for k in range(half - 1):
        stat_across.show([pair], sa, from_exp(k), par)
    for e in range(experts):
        weight_grad(gwout, e, hidden, g_rows)
    pg = pre_grad.astype(BF16)
    weight_grad(gwin, 0, x_rows, pg)
    forward.arrived()
    forward = [net.group(so_ag.at[0, 0]).show([peer], so_ag, par, s) for peer in seq_peers]
    columns = net.group(so_ag.at[0]).show([pair], so_ag, par, s)
    backward.arrived()
    piece = add_up([se[t] for t in range(seq_n)]).astype(BF16)
    sig_ag[h, par] = piece
    inner = jnp.sum(piece.astype(F32) * x_rows, axis=1, keepdims=True)
    si[h, par] = stat_tile(by_clip(inner, clips))
    along = [net.group(sig_ag.at[0, 0]).show([peer], sig_ag, h, par) for peer in exp_peers]
    inner_along = net.group(si.at[pl.ds(0, half - 1), 0]).show(exp_peers, si, h, par)
    across = net.group(sig_ag.at[pl.ds(0, half), 0]).show([pair], sig_ag, h, par)
    inner_across = net.group(si.at[pl.ds(0, half), 0]).show([pair], si, h, par)
    for e in range(1, experts):
        weight_grad(gwin, e, x_rows, pg)
    for k in range(seq_n - 1):
        forward[k].arrived()
        columns.show([pair], so_ag, par, (s + seq_n - 1 - k) % seq_n)
    for k in range(half - 1):
        along[k].arrived()
        across.show([pair], sig_ag, from_exp(k), par)
    inner_along.arrived()
    for k in range(half - 1):
        inner_across.show([pair], si, from_exp(k), par)

    def of_clip(value, c):
        return value.reshape(exp_n, clips, owned, value.shape[-1])[:, c].reshape(slots, value.shape[-1])

    def spread(value, c):
        value = value.reshape(exp_n, 1, owned, value.shape[-1])
        zero = jnp.zeros_like(value)
        parts = [value if k == c else zero for k in range(clips)]
        return jnp.concatenate(parts, axis=1).reshape(clips * slots, value.shape[-1])

    stat_across.arrived()
    columns.arrived()
    owners = [(g, q) for g in range(half) for q in range(2)]
    so = jnp.concatenate(
        [jnp.concatenate([so_ag[q, t, g] for t in range(seq_n)], axis=1) for g, q in owners], axis=0
    )
    stats = sa[...].reshape(slots, 128)
    for c in range(clips):
        mixing = qf[c]
        mixing_grad = of_clip(dot_nt(so, gout[c]), c)
        lm[c] = mixing * (mixing_grad - jnp.sum(mixing * mixing_grad, axis=0, keepdims=True))
        mass = stats[:, clips + c : clips + c + 1]
        dsp[c] = jnp.exp(lg[c] - stats[:, c : c + 1]) / mass
    across.arrived()
    inner_across.arrived()
    sig = sig_ag[...].reshape(exp_n * nr, width)
    inners = si[...].reshape(slots, 128)
    gr = 0.0
    for c in range(clips):
        dispatch_grad = of_clip(dot_nt(sig, tok[c]), c)
        lgrad = dsp[c] * (dispatch_grad - inners[:, c : c + 1]) + lm[c]
        lm[c] = lgrad
        gr = gr + dot(lgrad.astype(BF16), tok[c])

    out_rows = gr_o.shape[0]
    packed = gr_b.shape[2]
    pack = out_rows // packed
    whole = gr.T
    for t in range(seq_n):
        for g in range(half):
            for q in range(2):
                at = (t * exp_n + 2 * g + q) * out_rows
                parts = [whole[at + j * packed : at + (j + 1) * packed] for j in range(pack)]
                gr_a[q, t, g] = jnp.concatenate(parts, axis=1).astype(BF16)
    last = net.group(gr_p).start(gr_a.at[1 - par], gr_p, pair)
    both = jnp.concatenate([rt[...], sig], axis=0)

    def token_grad(c):
        left = jnp.concatenate([lm[c], spread(dsp[c], c)], axis=0)
        gt[c] = dot(left.T.astype(BF16), both).astype(BF16)

    last.arrived()
    gr_b[...] = (gr_a[par].astype(F32) + gr_p[...].astype(F32)).astype(BF16)
    last = net.group(gr_r)
    for k, (t, g) in enumerate(there):
        last.start(gr_b.at[t, g], gr_r.at[k], far_peers[k])
    for c in range(clips):
        mixed[c] = dot(spread(qf[c], c).T.astype(BF16), so).astype(BF16)
        token_grad(c)
    total = gr_b[s, h].astype(F32)
    last.arrived()
    for k in range(len(there)):
        total = total + gr_r[k].astype(F32)
    for j in range(pack):
        gr_o[j * packed : (j + 1) * packed] = total[:, j * slots : (j + 1) * slots]
    net.drain()
    assert len(net.groups) == groups_of(seq_n, exp_n)


def put_out(n, *refs):
    ins, outs, sem = refs[:n], refs[n : 2 * n], refs[2 * n]
    copies = []
    for src, dst in zip(ins, outs):
        copies.append(pltpu.make_async_copy(src, dst, sem.at[len(copies)]))
        copies[-1].start()
    for copy in copies:
        copy.wait()


def on_device(seq_n, exp_n, tokens, router, w_in, w_out, grad_out):
    clips, rows, width = tokens.shape
    slots = router.shape[1]
    half = exp_n // 2
    owned = slots // exp_n
    nr = clips * owned
    vmem = pl.BlockSpec(memory_space=pltpu.VMEM)
    hbm = pl.BlockSpec(memory_space=pltpu.HBM)
    anywhere = pl.BlockSpec(memory_space=pl.ANY)
    shape = jax.ShapeDtypeStruct
    out_rows = width // (seq_n * exp_n)
    pack = max(1, 128 // slots)
    tile = (out_rows // pack, slots * pack)
    piece = (nr, width)
    part = (nr, width // seq_n)
    stat = (owned, 128)
    n_groups = groups_of(seq_n, exp_n)
    outs = (
        shape(tokens.shape, BF16),
        shape(tokens.shape, BF16),
        shape(w_in.shape, BF16),
        shape(w_out.shape, BF16),
        shape((out_rows, slots), F32),
    )
    limit = VMEM_BYTES // 2
    results = pl.pallas_call(
        functools.partial(layer, seq_n, exp_n),
        out_shape=outs,
        in_specs=[hbm] * 5,
        out_specs=(vmem,) * 5,
        scratch_shapes=[
            pltpu.VMEM(tokens.shape, BF16),
            pltpu.VMEM(tokens.shape, BF16),
            pltpu.VMEM((slots, width), BF16),
            pltpu.VMEM(w_in.shape, BF16),
            pltpu.VMEM(w_out.shape, BF16),
            pltpu.VMEM((clips, slots, rows), F32),
            pltpu.VMEM((clips, slots, rows), F32),
            pltpu.VMEM((clips, slots, rows), F32),
            pltpu.VMEM((clips, slots, rows), F32),
            pltpu.VMEM((clips, slots, rows), BF16),
            pltpu.VMEM((clips, slots, rows), BF16),
            pltpu.VMEM((2, 2, half) + piece, BF16),
            pltpu.VMEM((2, half) + piece, BF16),
            pltpu.VMEM((half,) + piece, BF16),
            pltpu.VMEM((half - 1,) + piece, BF16),
            pltpu.VMEM((seq_n,) + piece, BF16),
            pltpu.VMEM((seq_n, half) + part, BF16),
            pltpu.VMEM((seq_n - 1, half) + part, BF16),
            pltpu.VMEM((half,) + part, BF16),
            pltpu.VMEM((half - 1,) + part, BF16),
            pltpu.VMEM((seq_n,) + part, BF16),
            pltpu.VMEM((seq_n,) + part, BF16),
            pltpu.VMEM((seq_n - 1,) + part, BF16),
            pltpu.VMEM((seq_n,) + piece, BF16),
            pltpu.VMEM((2, seq_n, half) + part, BF16),
            pltpu.VMEM((half, 2) + piece, BF16),
            pltpu.VMEM((2, half) + stat, F32),
            pltpu.VMEM((half,) + stat, F32),
            pltpu.VMEM((half,) + stat, F32),
            pltpu.VMEM((half - 1,) + stat, F32),
            pltpu.VMEM((seq_n,) + stat, F32),
            pltpu.VMEM((half, 2) + stat, F32),
            pltpu.VMEM((half, 2) + stat, F32),
            pltpu.VMEM((2, seq_n, half) + tile, BF16),
            pltpu.VMEM((seq_n, half) + tile, BF16),
            pltpu.VMEM((seq_n, half) + tile, BF16),
            pltpu.VMEM((seq_n * half - 1,) + tile, BF16),
            pltpu.SemaphoreType.DMA((2 * clips + 3,)),
            pltpu.SemaphoreType.DMA((n_groups,)),
            pltpu.SemaphoreType.DMA((n_groups,)),
        ],
        compiler_params=pltpu.CompilerParams(
            collective_id=0, has_side_effects=True, vmem_limit_bytes=limit
        ),
        name="layer",
    )(*[pltpu.with_memory_space_constraint(a, pltpu.HBM) for a in (tokens, router.T, grad_out, w_in, w_out)])
    mixed, grad_tokens, grad_w_in, grad_w_out, grad_router = pl.pallas_call(
        functools.partial(put_out, len(outs)),
        out_shape=outs,
        in_specs=[anywhere] * len(outs),
        out_specs=(hbm,) * len(outs),
        scratch_shapes=[pltpu.SemaphoreType.DMA((len(outs),))],
        compiler_params=pltpu.CompilerParams(vmem_limit_bytes=2**20),
        name="put_out",
    )(*results)
    return mixed, grad_tokens, grad_router, grad_w_in, grad_w_out


def solution(mesh):
    return jax.shard_map(
        functools.partial(on_device, mesh.shape["seq"], mesh.shape["exp"]),
        mesh=mesh,
        in_specs=(
            P(None, ("seq", "exp"), None),
            P(),
            P("exp", None, "seq"),
            P("exp", "seq", None),
            P(None, ("seq", "exp"), None),
        ),
        out_specs=(
            P(None, ("seq", "exp"), None),
            P(None, ("seq", "exp"), None),
            P(("seq", "exp"), None),
            P("exp", None, "seq"),
            P("exp", "seq", None),
        ),
        check_vma=False,
    )
```

time: 49.2 us -> 46.5 us (0.945)
  Pallas kernels: 48.4 us -> 45.8 us
    pallas_call x1, Pallas kernels: 43 us -> 40.4 us  [on_device(): pl.pallas_call(functools.partial(layer, seq_n, exp_n), out_shape=outs, in...]
where the time goes in v3:
time: 46.5 us; the launch traced here: 46.4 us
  Pallas kernels  45.8 us (98%)
  between operations  0.64 us (1%)
    pallas_call x1, Pallas kernels, on_device(): pl.pallas_call(functools.partial(layer, seq_n, exp_n), out_shape=outs, in...  40.4 us
    pallas_call x1, Pallas kernels, on_device(): pl.pallas_call(functools.partial(put_out, len(outs)), out_shape=outs, in_...  5.39 us

profile of v3, /device:TPU:0, one launch (start us, length us, event | category | flops | bytes accessed | tf_op | source)
XLA Modules:
  0.0 46.4 jit_solution(17831534912867471045)
XLA Ops:
  0.6 40.4 %layer.1 = (bf16[2,768,1024]{2,1,0:T(8,128)(2,1)S(1)}, bf16[2,768,1024]{2,1,0:T(8,128)(2,1)S(1)}, bf16[2,1024,1024]{2,1,0:T(8,128)(2,1)S(1)}, bf16[2,1024,1024]{2,1,0:T(8,128)(2,1)S(1)}, f32[32,64]{1,0:T(8,128)S(1)}) custom-call(bf16[2,768,1024]{2,1,0:T(8,128)(2,1)} %tok_hbm.1, bf16[64,1024]{1,0:T(8,128)(2,1)} %bitcast.1, bf16[2,768,1024]{2,1,0:T(8,128)(2,1)} %gout_hbm.1, ...), custom_call_target="tpu_custom_call" | custom-call | tf_op jit(solution)/shard_map/layer/pallas_call | solution.py:422
  41.0 5.4 %put_out.1 = (bf16[2,768,1024]{2,1,0:T(8,128)(2,1)}, bf16[2,768,1024]{2,1,0:T(8,128)(2,1)}, bf16[2,1024,1024]{2,1,0:T(8,128)(2,1)}, bf16[2,1024,1024]{2,1,0:T(8,128)(2,1)}, f32[32,64]{1,0:T(8,128)}) custom-call(bf16[2,768,1024]{2,1,0:T(8,128)(2,1)S(1)} %get-tuple-element.15.refs_0_, bf16[2,768,1024]{2,1,0:T(8,128)(2,1)S(1)} %get-tuple-element.16.refs_1_, ...), custom_call_target="tpu_custom_call" | custom-call | tf_op jit(solution)/shard_map/put_out/pallas_call | solution.py:474

commit v4 on v3

--- a/solution.py
+++ b/solution.py
@@ -109,7 +109,7 @@
 def layer(
     seq_n, exp_n, tok_hbm, rt_hbm, gout_hbm, win_hbm, wout_hbm,
     mixed, gt, gwin, gwout, gr_o,
-    tok, gout, rt, win, wout, lg, qf, dsp, lm, xt, qt,
+    tok, gout, rt, win, wout, tok_t, gout_t, win_t, wout_t, lg, qf, dsp, lm, xt, qt,
     buf_a, rcv_a, xb, xr, xg, gb, gbr, gc, gcr, gg, fe, fer, se, so_ag, sig_ag,
     st_a, st_p, st_b, st_z, st_c, sa, si,
     gr_a, gr_p, gr_b, gr_r,
@@ -133,7 +133,7 @@
     load_in = pltpu.make_async_copy(win_hbm, win, w_sem.at[1 + 2 * clips])
     load_out = pltpu.make_async_copy(wout_hbm, wout, w_sem.at[2 + 2 * clips])
     load_rt.start()
-    for load in load_tok:
+    for load in load_tok + load_gout:
         load.start()
     barrier = pltpu.get_barrier_semaphore()
     for peer in [pair] + far_peers:
@@ -144,7 +144,6 @@
     values, peaks, masses = [], [], []
     for c in range(clips):
         load_tok[c].wait()
-        load_gout[c].start()
         values.append(dot_nt(rt[...], tok[c]))
     for c, value in enumerate(values):
         lg[c] = value
@@ -225,6 +224,9 @@
         for t in range(seq_n):
             gb[t, g] = value[:, t * dc : (t + 1) * dc]
     grads = spread_over(seq_peers, seq_of, gb, gbr)
+    for c in range(clips):
+        tok_t[c] = tok[c].T
+        gout_t[c] = gout[c].T
     stat.arrived()
     parts = [split_stats(st_b[h], clips)] + [split_stats(st_z[k], clips) for k in range(half - 1)]
     peak, mass, fac = join(parts)
@@ -237,6 +239,12 @@
     inputs.arrived()
     xg[s] = add_up([xb[h]] + [xr[k] for k in range(half - 1)], fac).astype(BF16)
     inputs = show_seq(xg)
+    load_out.wait()
+    load_in.wait()
+    for e in range(experts):
+        wout_t[e] = wout[e].T
+    for e in range(experts // 2):
+        win_t[e] = win[e].T
     stat.arrived()
     peak, mass, fac = join([split_stats(st_c[t], clips) for t in range(seq_n)])
     fac = [f / mass for f in fac]
@@ -250,8 +258,6 @@
     row = lax.broadcasted_iota(jnp.int32, (nr, 1), 0)
     expert_of = (row % owned) // (owned // experts)
     mask = [(expert_of == e).astype(F32) for e in range(experts)]
-    load_out.wait()
-    load_in.wait()
     inputs.arrived()
     x_rows = add_up([xg[t] for t in range(seq_n)], fac)
     pre = 0.0
@@ -264,15 +270,17 @@
     for t in range(seq_n):
         fe[t] = out_part[:, t * dc : (t + 1) * dc].astype(BF16)
     forward = spread_over(seq_peers, seq_of, fe, fer)
+    for e in range(experts // 2, experts):
+        win_t[e] = win[e].T
     grads.arrived()
     g_rows = jnp.concatenate([gg[t] for t in range(seq_n)], axis=1)
     hidden_grad = 0.0
     for e in range(experts):
-        hidden_grad = hidden_grad + dot_nt(g_rows, wout[e]) * mask[e]
+        hidden_grad = hidden_grad + dot(g_rows, wout_t[e]) * mask[e]
     pre_grad = back(hidden_grad)[0]
     in_part = 0.0
     for e in range(experts):
-        in_part = in_part + dot_nt((pre_grad * mask[e]).astype(BF16), win[e])
+        in_part = in_part + dot((pre_grad * mask[e]).astype(BF16), win_t[e])
     se[s] = in_part.astype(BF16)
     backward = show_seq(se)
 
@@ -334,7 +342,7 @@
     stats = sa[...].reshape(slots, 128)
     for c in range(clips):
         mixing = qf[c]
-        mixing_grad = of_clip(dot_nt(so, gout[c]), c)
+        mixing_grad = of_clip(dot(so, gout_t[c]), c)
         lm[c] = mixing * (mixing_grad - jnp.sum(mixing * mixing_grad, axis=0, keepdims=True))
         mass = stats[:, clips + c : clips + c + 1]
         dsp[c] = jnp.exp(lg[c] - stats[:, c : c + 1]) / mass
@@ -344,7 +352,7 @@
     inners = si[...].reshape(slots, 128)
     gr = 0.0
     for c in range(clips):
-        dispatch_grad = of_clip(dot_nt(sig, tok[c]), c)
+        dispatch_grad = of_clip(dot(sig, tok_t[c]), c)
         lgrad = dsp[c] * (dispatch_grad - inners[:, c : c + 1]) + lm[c]
         lm[c] = lgrad
         gr = gr + dot(lgrad.astype(BF16), tok[c])
@@ -397,6 +405,7 @@
 def on_device(seq_n, exp_n, tokens, router, w_in, w_out, grad_out):
     clips, rows, width = tokens.shape
     slots = router.shape[1]
+    experts, _, ff = w_in.shape
     half = exp_n // 2
     owned = slots // exp_n
     nr = clips * owned
@@ -418,7 +427,7 @@
         shape(w_out.shape, BF16),
         shape((out_rows, slots), F32),
     )
-    limit = VMEM_BYTES // 2
+    limit = VMEM_BYTES // 16 * 9
     results = pl.pallas_call(
         functools.partial(layer, seq_n, exp_n),
         out_shape=outs,
@@ -430,6 +439,10 @@
             pltpu.VMEM((slots, width), BF16),
             pltpu.VMEM(w_in.shape, BF16),
             pltpu.VMEM(w_out.shape, BF16),
+            pltpu.VMEM((clips, width, rows), BF16),
+            pltpu.VMEM((clips, width, rows), BF16),
+            pltpu.VMEM((experts, ff, width), BF16),
+            pltpu.VMEM((experts, width, ff), BF16),
             pltpu.VMEM((clips, slots, rows), F32),
             pltpu.VMEM((clips, slots, rows), F32),
             pltpu.VMEM((clips, slots, rows), F32),

time: 46.5 us -> 44.6 us (0.959)
  Pallas kernels: 45.8 us -> 43.8 us
    pallas_call x1, Pallas kernels: 40.4 us -> 38.4 us  [on_device(): pl.pallas_call(functools.partial(layer, seq_n, exp_n), out_shape=outs, in...]
where the time goes in v4:
time: 44.6 us; the launch traced here: 44.4 us
  Pallas kernels  43.8 us (98%)
  between operations  0.64 us (1%)
    pallas_call x1, Pallas kernels, on_device(): pl.pallas_call(functools.partial(layer, seq_n, exp_n), out_shape=outs, in...  38.4 us
    pallas_call x1, Pallas kernels, on_device(): pl.pallas_call(functools.partial(put_out, len(outs)), out_shape=outs, in_...  5.39 us

profile of v4, /device:TPU:0, one launch (start us, length us, event | category | flops | bytes accessed | tf_op | source)
XLA Modules:
  0.0 44.4 jit_solution(311545049547994604)
XLA Ops:
  0.6 38.4 %layer.1 = (bf16[2,768,1024]{2,1,0:T(8,128)(2,1)S(1)}, bf16[2,768,1024]{2,1,0:T(8,128)(2,1)S(1)}, bf16[2,1024,1024]{2,1,0:T(8,128)(2,1)S(1)}, bf16[2,1024,1024]{2,1,0:T(8,128)(2,1)S(1)}, f32[32,64]{1,0:T(8,128)S(1)}) custom-call(bf16[2,768,1024]{2,1,0:T(8,128)(2,1)} %tok_hbm.1, bf16[64,1024]{1,0:T(8,128)(2,1)} %bitcast.1, bf16[2,768,1024]{2,1,0:T(8,128)(2,1)} %gout_hbm.1, ...), custom_call_target="tpu_custom_call" | custom-call | tf_op jit(solution)/shard_map/layer/pallas_call | solution.py:431
  39.0 5.4 %put_out.1 = (bf16[2,768,1024]{2,1,0:T(8,128)(2,1)}, bf16[2,768,1024]{2,1,0:T(8,128)(2,1)}, bf16[2,1024,1024]{2,1,0:T(8,128)(2,1)}, bf16[2,1024,1024]{2,1,0:T(8,128)(2,1)}, f32[32,64]{1,0:T(8,128)}) custom-call(bf16[2,768,1024]{2,1,0:T(8,128)(2,1)S(1)} %get-tuple-element.15.refs_0_, bf16[2,768,1024]{2,1,0:T(8,128)(2,1)S(1)} %get-tuple-element.16.refs_1_, ...), custom_call_target="tpu_custom_call" | custom-call | tf_op jit(solution)/shard_map/put_out/pallas_call | solution.py:487

commit v5 on v4

--- a/solution.py
+++ b/solution.py
@@ -30,8 +30,9 @@
     pair = (s, h * 2 + (1 - par))
     seq_peers = [((s + k) % seq_n, e) for k in range(1, seq_n)]
     exp_peers = [(s, ((h + k) % half) * 2 + par) for k in range(1, half)]
-    there = [((s + a) % seq_n, (h + b) % half) for a in range(seq_n) for b in range(half) if a or b]
-    return s, h, par, pair, seq_peers, exp_peers, there
+    ways = [(a, b) for a in range(seq_n) for b in range(half) if a or b]
+    there = [((s + a) % seq_n, (h + b) % half) for a, b in ways]
+    return s, h, par, pair, seq_peers, exp_peers, ways, there
 
 
 class Net:
@@ -122,16 +123,18 @@
     nr = clips * owned
     dc = width // seq_n
     experts = win.shape[0]
-    s, h, par, pair, seq_peers, exp_peers, there = place(seq_n, exp_n)
+    s, h, par, pair, seq_peers, exp_peers, ways, there = place(seq_n, exp_n)
     far_peers = [(t, g * 2 + par) for t, g in there]
 
     load_rt = pltpu.make_async_copy(rt_hbm, rt, w_sem.at[0])
-    load_tok = [pltpu.make_async_copy(tok_hbm.at[c], tok.at[c], w_sem.at[1 + c]) for c in range(clips)]
+    load_tok = [
+        pltpu.make_async_copy(tok_hbm.at[c], tok.at[c], w_sem.at[3 + clips + c]) for c in range(clips)
+    ]
     load_gout = [
-        pltpu.make_async_copy(gout_hbm.at[c], gout.at[c], w_sem.at[1 + clips + c]) for c in range(clips)
+        pltpu.make_async_copy(gout_hbm.at[c], gout.at[c], w_sem.at[1 + c]) for c in range(clips)
     ]
-    load_in = pltpu.make_async_copy(win_hbm, win, w_sem.at[1 + 2 * clips])
-    load_out = pltpu.make_async_copy(wout_hbm, wout, w_sem.at[2 + 2 * clips])
+    load_in = pltpu.make_async_copy(win_hbm, win, w_sem.at[1 + clips])
+    load_out = pltpu.make_async_copy(wout_hbm, wout, w_sem.at[2 + clips])
     load_rt.start()
     for load in load_tok + load_gout:
         load.start()
@@ -254,6 +257,8 @@
     grads.arrived()
     gg[s] = add_up([gc[h]] + [gcr[k] for k in range(half - 1)]).astype(BF16)
     grads = show_seq(gg)
+    for e in range(experts // 2, experts):
+        win_t[e] = win[e].T
 
     row = lax.broadcasted_iota(jnp.int32, (nr, 1), 0)
     expert_of = (row % owned) // (owned // experts)
@@ -270,8 +275,6 @@
     for t in range(seq_n):
         fe[t] = out_part[:, t * dc : (t + 1) * dc].astype(BF16)
     forward = spread_over(seq_peers, seq_of, fe, fer)
-    for e in range(experts // 2, experts):
-        win_t[e] = win[e].T
     grads.arrived()
     g_rows = jnp.concatenate([gg[t] for t in range(seq_n)], axis=1)
     hidden_grad = 0.0
@@ -290,39 +293,42 @@
     def weight_grad(out, e, left, right):
         out[e] = dot((left * mask[e]).T.astype(BF16), right).astype(BF16)
 
+    weight_grad(gwout, 0, hidden, g_rows)
     forward.arrived()
     so_ag[par, s, h] = add_up([fe[s]] + [fer[k] for k in range(seq_n - 1)]).astype(BF16)
-    forward = net.group(so_ag.at[0, 0, pl.ds(0, half - 1)]).show(exp_peers, so_ag, par, s, h)
+    forward = []
+    for a in range(seq_n):
+        here = [peer for way, peer in zip(ways, far_peers) if way[0] == a]
+        group = net.group(so_ag.at[0, 0, pl.ds(0, len(here))])
+        group.show(here, so_ag, par, s, h)
+        forward.append(group)
+    columns = net.group(so_ag.at[0])
     stat_along.arrived()
     for k in range(half - 1):
         stat_across.show([pair], sa, from_exp(k), par)
-    for e in range(experts):
+    for e in range(1, experts):
         weight_grad(gwout, e, hidden, g_rows)
     pg = pre_grad.astype(BF16)
-    weight_grad(gwin, 0, x_rows, pg)
-    forward.arrived()
-    forward = [net.group(so_ag.at[0, 0]).show([peer], so_ag, par, s) for peer in seq_peers]
-    columns = net.group(so_ag.at[0]).show([pair], so_ag, par, s)
     backward.arrived()
     piece = add_up([se[t] for t in range(seq_n)]).astype(BF16)
     sig_ag[h, par] = piece
     inner = jnp.sum(piece.astype(F32) * x_rows, axis=1, keepdims=True)
     si[h, par] = stat_tile(by_clip(inner, clips))
+    inner_along = net.group(si.at[pl.ds(0, half - 1), 0]).show(exp_peers, si, h, par)
     along = [net.group(sig_ag.at[0, 0]).show([peer], sig_ag, h, par) for peer in exp_peers]
-    inner_along = net.group(si.at[pl.ds(0, half - 1), 0]).show(exp_peers, si, h, par)
+    inner_across = net.group(si.at[pl.ds(0, half), 0]).show([pair], si, h, par)
     across = net.group(sig_ag.at[pl.ds(0, half), 0]).show([pair], sig_ag, h, par)
-    inner_across = net.group(si.at[pl.ds(0, half), 0]).show([pair], si, h, par)
-    for e in range(1, experts):
+    for e in range(experts):
         weight_grad(gwin, e, x_rows, pg)
-    for k in range(seq_n - 1):
-        forward[k].arrived()
-        columns.show([pair], so_ag, par, (s + seq_n - 1 - k) % seq_n)
+    for a in range(seq_n):
+        forward[a].arrived()
+        columns.show([pair], so_ag, par, (s + seq_n - a) % seq_n)
+    inner_along.arrived()
+    for k in range(half - 1):
+        inner_across.show([pair], si, from_exp(k), par)
     for k in range(half - 1):
         along[k].arrived()
         across.show([pair], sig_ag, from_exp(k), par)
-    inner_along.arrived()
-    for k in range(half - 1):
-        inner_across.show([pair], si, from_exp(k), par)
 
     def of_clip(value, c):
         return value.reshape(exp_n, clips, owned, value.shape[-1])[:, c].reshape(slots, value.shape[-1])

time: 44.6 us -> 44.2 us (level)
  no operation moved by 1% of the time
where the time goes in v5:
time: 44.2 us; the launch traced here: 44 us
  Pallas kernels  43.4 us (98%)
  between operations  0.64 us (1%)
    pallas_call x1, Pallas kernels, on_device(): pl.pallas_call(functools.partial(layer, seq_n, exp_n), out_shape=outs, in...  38 us
    pallas_call x1, Pallas kernels, on_device(): pl.pallas_call(functools.partial(put_out, len(outs)), out_shape=outs, in_...  5.39 us

profile of v5, /device:TPU:0, one launch (start us, length us, event | category | flops | bytes accessed | tf_op | source)
XLA Modules:
  0.0 44.0 jit_solution(12090067275534781443)
XLA Ops:
  0.6 38.0 %layer.1 = (bf16[2,768,1024]{2,1,0:T(8,128)(2,1)S(1)}, bf16[2,768,1024]{2,1,0:T(8,128)(2,1)S(1)}, bf16[2,1024,1024]{2,1,0:T(8,128)(2,1)S(1)}, bf16[2,1024,1024]{2,1,0:T(8,128)(2,1)S(1)}, f32[32,64]{1,0:T(8,128)S(1)}) custom-call(bf16[2,768,1024]{2,1,0:T(8,128)(2,1)} %tok_hbm.1, bf16[64,1024]{1,0:T(8,128)(2,1)} %bitcast.1, bf16[2,768,1024]{2,1,0:T(8,128)(2,1)} %gout_hbm.1, ...), custom_call_target="tpu_custom_call" | custom-call | tf_op jit(solution)/shard_map/layer/pallas_call | solution.py:437
  38.6 5.4 %put_out.1 = (bf16[2,768,1024]{2,1,0:T(8,128)(2,1)}, bf16[2,768,1024]{2,1,0:T(8,128)(2,1)}, bf16[2,1024,1024]{2,1,0:T(8,128)(2,1)}, bf16[2,1024,1024]{2,1,0:T(8,128)(2,1)}, f32[32,64]{1,0:T(8,128)}) custom-call(bf16[2,768,1024]{2,1,0:T(8,128)(2,1)S(1)} %get-tuple-element.15.refs_0_, bf16[2,768,1024]{2,1,0:T(8,128)(2,1)S(1)} %get-tuple-element.16.refs_1_, ...), custom_call_target="tpu_custom_call" | custom-call | tf_op jit(solution)/shard_map/put_out/pallas_call | solution.py:493

commit v6 on v5

--- a/solution.py
+++ b/solution.py
@@ -73,7 +73,7 @@
 
 
 def groups_of(seq_n, exp_n):
-    return 21 + (seq_n - 1) + (exp_n // 2 - 1)
+    return 23 + (seq_n - 1) + 2 * (exp_n // 2 - 1)
 
 
 def stat_tile(columns):
@@ -122,6 +122,7 @@
     owned = slots // exp_n
     nr = clips * owned
     dc = width // seq_n
+    cuts = [slice(j * (width // 2), (j + 1) * (width // 2)) for j in range(2)]
     experts = win.shape[0]
     s, h, par, pair, seq_peers, exp_peers, ways, there = place(seq_n, exp_n)
     far_peers = [(t, g * 2 + par) for t, g in there]
@@ -239,11 +240,13 @@
     for g in range(half):
         gc[g] = add_up([gb[s, g]] + [gbr[k, g] for k in range(seq_n - 1)]).astype(BF16)
     grads = spread_over(exp_peers, exp_of, gc, gcr)
+    load_out.wait()
+    load_in.wait()
+    for e in range(experts // 2, experts):
+        win_t[e] = win[e].T
     inputs.arrived()
     xg[s] = add_up([xb[h]] + [xr[k] for k in range(half - 1)], fac).astype(BF16)
     inputs = show_seq(xg)
-    load_out.wait()
-    load_in.wait()
     for e in range(experts):
         wout_t[e] = wout[e].T
     for e in range(experts // 2):
@@ -257,8 +260,6 @@
     grads.arrived()
     gg[s] = add_up([gc[h]] + [gcr[k] for k in range(half - 1)]).astype(BF16)
     grads = show_seq(gg)
-    for e in range(experts // 2, experts):
-        win_t[e] = win[e].T
 
     row = lax.broadcasted_iota(jnp.int32, (nr, 1), 0)
     expert_of = (row % owned) // (owned // experts)
@@ -281,11 +282,13 @@
     for e in range(experts):
         hidden_grad = hidden_grad + dot(g_rows, wout_t[e]) * mask[e]
     pre_grad = back(hidden_grad)[0]
-    in_part = 0.0
-    for e in range(experts):
-        in_part = in_part + dot((pre_grad * mask[e]).astype(BF16), win_t[e])
-    se[s] = in_part.astype(BF16)
-    backward = show_seq(se)
+    backward = []
+    for j, cut in enumerate(cuts):
+        in_part = 0.0
+        for e in range(experts):
+            in_part = in_part + dot((pre_grad * mask[e]).astype(BF16), win_t[e, :, cut])
+        se[j, s] = in_part.astype(BF16)
+        backward.append(net.group(se.at[j, pl.ds(0, seq_n - 1)]).show(seq_peers, se, j, s))
 
     def from_exp(k):
         return (h + half - 1 - k) % half
@@ -309,26 +312,33 @@
     for e in range(1, experts):
         weight_grad(gwout, e, hidden, g_rows)
     pg = pre_grad.astype(BF16)
-    backward.arrived()
-    piece = add_up([se[t] for t in range(seq_n)]).astype(BF16)
-    sig_ag[h, par] = piece
-    inner = jnp.sum(piece.astype(F32) * x_rows, axis=1, keepdims=True)
-    si[h, par] = stat_tile(by_clip(inner, clips))
-    inner_along = net.group(si.at[pl.ds(0, half - 1), 0]).show(exp_peers, si, h, par)
-    along = [net.group(sig_ag.at[0, 0]).show([peer], sig_ag, h, par) for peer in exp_peers]
-    inner_across = net.group(si.at[pl.ds(0, half), 0]).show([pair], si, h, par)
-    across = net.group(sig_ag.at[pl.ds(0, half), 0]).show([pair], sig_ag, h, par)
+    inner, along, across = 0.0, [], []
+    for j, cut in enumerate(cuts):
+        backward[j].arrived()
+        piece = add_up([se[j, t] for t in range(seq_n)]).astype(BF16)
+        sig_ag[j, h, par] = piece
+        inner = inner + jnp.sum(piece.astype(F32) * x_rows[:, cut], axis=1, keepdims=True)
+        if j == len(cuts) - 1:
+            si[h, par] = stat_tile(by_clip(inner, clips))
+            inner_along = net.group(si.at[pl.ds(0, half - 1), 0]).show(exp_peers, si, h, par)
+            inner_across = net.group(si.at[pl.ds(0, half), 0]).show([pair], si, h, par)
+        along.append(
+            [net.group(sig_ag.at[0, 0, 0]).show([peer], sig_ag, j, h, par) for peer in exp_peers]
+        )
+        across.append(net.group(sig_ag.at[0, pl.ds(0, half), 0]).show([pair], sig_ag, j, h, par))
     for e in range(experts):
         weight_grad(gwin, e, x_rows, pg)
     for a in range(seq_n):
         forward[a].arrived()
         columns.show([pair], so_ag, par, (s + seq_n - a) % seq_n)
-    inner_along.arrived()
-    for k in range(half - 1):
-        inner_across.show([pair], si, from_exp(k), par)
-    for k in range(half - 1):
-        along[k].arrived()
-        across.show([pair], sig_ag, from_exp(k), par)
+    for j in range(len(cuts)):
+        if j == len(cuts) - 1:
+            inner_along.arrived()
+            for k in range(half - 1):
+                inner_across.show([pair], si, from_exp(k), par)
+        for k in range(half - 1):
+            along[j][k].arrived()
+            across[j].show([pair], sig_ag, j, from_exp(k), par)
 
     def of_clip(value, c):
         return value.reshape(exp_n, clips, owned, value.shape[-1])[:, c].reshape(slots, value.shape[-1])
@@ -352,9 +362,12 @@
         lm[c] = mixing * (mixing_grad - jnp.sum(mixing * mixing_grad, axis=0, keepdims=True))
         mass = stats[:, clips + c : clips + c + 1]
         dsp[c] = jnp.exp(lg[c] - stats[:, c : c + 1]) / mass
-    across.arrived()
+    for j in range(len(cuts)):
+        across[j].arrived()
     inner_across.arrived()
-    sig = sig_ag[...].reshape(exp_n * nr, width)
+    sig = jnp.concatenate(
+        [sig_ag[j].reshape(exp_n * nr, width // len(cuts)) for j in range(len(cuts))], axis=1
+    )
     inners = si[...].reshape(slots, 128)
     gr = 0.0
     for c in range(clips):
@@ -467,9 +480,9 @@
             pltpu.VMEM((seq_n,) + part, BF16),
             pltpu.VMEM((seq_n,) + part, BF16),
             pltpu.VMEM((seq_n - 1,) + part, BF16),
-            pltpu.VMEM((seq_n,) + piece, BF16),
+            pltpu.VMEM((2, seq_n, nr, width // 2), BF16),
             pltpu.VMEM((2, seq_n, half) + part, BF16),
-            pltpu.VMEM((half, 2) + piece, BF16),
+            pltpu.VMEM((2, half, 2, nr, width // 2), BF16),
             pltpu.VMEM((2, half) + stat, F32),
             pltpu.VMEM((half,) + stat, F32),
             pltpu.VMEM((half,) + stat, F32),

time: 44.2 us -> 43.9 us (level)
  no operation moved by 1% of the time
where the time goes in v6:
time: 43.9 us; the launch traced here: 43.8 us
  Pallas kernels  43 us (98%)
  between operations  0.8 us (2%)
    pallas_call x1, Pallas kernels, on_device(): pl.pallas_call(functools.partial(layer, seq_n, exp_n), out_shape=outs, in...  37.6 us
    pallas_call x1, Pallas kernels, on_device(): pl.pallas_call(functools.partial(put_out, len(outs)), out_shape=outs, in_...  5.39 us

profile of v6, /device:TPU:0, one launch (start us, length us, event | category | flops | bytes accessed | tf_op | source)
XLA Modules:
  0.0 43.8 jit_solution(9638941138742550245)
XLA Ops:
  0.6 37.6 %layer.1 = (bf16[2,768,1024]{2,1,0:T(8,128)(2,1)S(1)}, bf16[2,768,1024]{2,1,0:T(8,128)(2,1)S(1)}, bf16[2,1024,1024]{2,1,0:T(8,128)(2,1)S(1)}, bf16[2,1024,1024]{2,1,0:T(8,128)(2,1)S(1)}, f32[32,64]{1,0:T(8,128)S(1)}) custom-call(bf16[2,768,1024]{2,1,0:T(8,128)(2,1)} %tok_hbm.1, bf16[64,1024]{1,0:T(8,128)(2,1)} %bitcast.1, bf16[2,768,1024]{2,1,0:T(8,128)(2,1)} %gout_hbm.1, ...), custom_call_target="tpu_custom_call" | custom-call | tf_op jit(solution)/shard_map/layer/pallas_call | solution.py:450
  38.2 5.4 %put_out.1 = (bf16[2,768,1024]{2,1,0:T(8,128)(2,1)}, bf16[2,768,1024]{2,1,0:T(8,128)(2,1)}, bf16[2,1024,1024]{2,1,0:T(8,128)(2,1)}, bf16[2,1024,1024]{2,1,0:T(8,128)(2,1)}, f32[32,64]{1,0:T(8,128)}) custom-call(bf16[2,768,1024]{2,1,0:T(8,128)(2,1)S(1)} %get-tuple-element.15.refs_0_, bf16[2,768,1024]{2,1,0:T(8,128)(2,1)S(1)} %get-tuple-element.16.refs_1_, ...), custom_call_target="tpu_custom_call" | custom-call | tf_op jit(solution)/shard_map/put_out/pallas_call | solution.py:506

commit v7 on v6

--- a/solution.py
+++ b/solution.py
@@ -287,8 +287,9 @@
         in_part = 0.0
         for e in range(experts):
             in_part = in_part + dot((pre_grad * mask[e]).astype(BF16), win_t[e, :, cut])
-        se[j, s] = in_part.astype(BF16)
-        backward.append(net.group(se.at[j, pl.ds(0, seq_n - 1)]).show(seq_peers, se, j, s))
+        se[s, :, cut] = in_part.astype(BF16)
+        whole = net.group(se.at[pl.ds(0, seq_n - 1), :, cut])
+        backward.append(whole.show(seq_peers, se, s, slice(None), cut))
 
     def from_exp(k):
         return (h + half - 1 - k) % half
@@ -315,30 +316,29 @@
     inner, along, across = 0.0, [], []
     for j, cut in enumerate(cuts):
         backward[j].arrived()
-        piece = add_up([se[j, t] for t in range(seq_n)]).astype(BF16)
-        sig_ag[j, h, par] = piece
+        piece = add_up([se[t, :, cut] for t in range(seq_n)]).astype(BF16)
+        sig_ag[h, par, :, cut] = piece
         inner = inner + jnp.sum(piece.astype(F32) * x_rows[:, cut], axis=1, keepdims=True)
         if j == len(cuts) - 1:
             si[h, par] = stat_tile(by_clip(inner, clips))
             inner_along = net.group(si.at[pl.ds(0, half - 1), 0]).show(exp_peers, si, h, par)
             inner_across = net.group(si.at[pl.ds(0, half), 0]).show([pair], si, h, par)
-        along.append(
-            [net.group(sig_ag.at[0, 0, 0]).show([peer], sig_ag, j, h, par) for peer in exp_peers]
-        )
-        across.append(net.group(sig_ag.at[0, pl.ds(0, half), 0]).show([pair], sig_ag, j, h, par))
+        at = (h, par, slice(None), cut)
+        along.append([net.group(sig_ag.at[0, 0, :, cut]).show([peer], sig_ag, *at) for peer in exp_peers])
+        across.append(net.group(sig_ag.at[pl.ds(0, half), 0, :, cut]).show([pair], sig_ag, *at))
     for e in range(experts):
         weight_grad(gwin, e, x_rows, pg)
     for a in range(seq_n):
         forward[a].arrived()
         columns.show([pair], so_ag, par, (s + seq_n - a) % seq_n)
-    for j in range(len(cuts)):
+    for j, cut in enumerate(cuts):
         if j == len(cuts) - 1:
             inner_along.arrived()
             for k in range(half - 1):
                 inner_across.show([pair], si, from_exp(k), par)
         for k in range(half - 1):
             along[j][k].arrived()
-            across[j].show([pair], sig_ag, j, from_exp(k), par)
+            across[j].show([pair], sig_ag, from_exp(k), par, slice(None), cut)
 
     def of_clip(value, c):
         return value.reshape(exp_n, clips, owned, value.shape[-1])[:, c].reshape(slots, value.shape[-1])
@@ -350,24 +350,23 @@
         return jnp.concatenate(parts, axis=1).reshape(clips * slots, value.shape[-1])
 
     stat_across.arrived()
+    stats = sa[...].reshape(slots, 128)
+    for c in range(clips):
+        mass = stats[:, clips + c : clips + c + 1]
+        dsp[c] = jnp.exp(lg[c] - stats[:, c : c + 1]) / mass
     columns.arrived()
     owners = [(g, q) for g in range(half) for q in range(2)]
     so = jnp.concatenate(
         [jnp.concatenate([so_ag[q, t, g] for t in range(seq_n)], axis=1) for g, q in owners], axis=0
     )
-    stats = sa[...].reshape(slots, 128)
     for c in range(clips):
         mixing = qf[c]
         mixing_grad = of_clip(dot(so, gout_t[c]), c)
         lm[c] = mixing * (mixing_grad - jnp.sum(mixing * mixing_grad, axis=0, keepdims=True))
-        mass = stats[:, clips + c : clips + c + 1]
-        dsp[c] = jnp.exp(lg[c] - stats[:, c : c + 1]) / mass
     for j in range(len(cuts)):
         across[j].arrived()
     inner_across.arrived()
-    sig = jnp.concatenate(
-        [sig_ag[j].reshape(exp_n * nr, width // len(cuts)) for j in range(len(cuts))], axis=1
-    )
+    sig = sig_ag[...].reshape(exp_n * nr, width)
     inners = si[...].reshape(slots, 128)
     gr = 0.0
     for c in range(clips):
@@ -480,9 +479,9 @@
             pltpu.VMEM((seq_n,) + part, BF16),
             pltpu.VMEM((seq_n,) + part, BF16),
             pltpu.VMEM((seq_n - 1,) + part, BF16),
-            pltpu.VMEM((2, seq_n, nr, width // 2), BF16),
+            pltpu.VMEM((seq_n,) + piece, BF16),
             pltpu.VMEM((2, seq_n, half) + part, BF16),
-            pltpu.VMEM((2, half, 2, nr, width // 2), BF16),
+            pltpu.VMEM((half, 2) + piece, BF16),
             pltpu.VMEM((2, half) + stat, F32),
             pltpu.VMEM((half,) + stat, F32),
             pltpu.VMEM((half,) + stat, F32),

time: 43.9 us -> 43.6 us (level)
  no operation moved by 1% of the time
where the time goes in v7:
time: 43.6 us; the launch traced here: 43.4 us
  Pallas kernels  42.8 us (98%)
  between operations  0.64 us (1%)
    pallas_call x1, Pallas kernels, on_device(): pl.pallas_call(functools.partial(layer, seq_n, exp_n), out_shape=outs, in...  37.4 us
    pallas_call x1, Pallas kernels, on_device(): pl.pallas_call(functools.partial(put_out, len(outs)), out_shape=outs, in_...  5.39 us

profile of v7, /device:TPU:0, one launch (start us, length us, event | category | flops | bytes accessed | tf_op | source)
XLA Modules:
  0.0 43.4 jit_solution(1863959412866568733)
XLA Ops:
  0.6 37.4 %layer.1 = (bf16[2,768,1024]{2,1,0:T(8,128)(2,1)S(1)}, bf16[2,768,1024]{2,1,0:T(8,128)(2,1)S(1)}, bf16[2,1024,1024]{2,1,0:T(8,128)(2,1)S(1)}, bf16[2,1024,1024]{2,1,0:T(8,128)(2,1)S(1)}, f32[32,64]{1,0:T(8,128)S(1)}) custom-call(bf16[2,768,1024]{2,1,0:T(8,128)(2,1)} %tok_hbm.1, bf16[64,1024]{1,0:T(8,128)(2,1)} %bitcast.1, bf16[2,768,1024]{2,1,0:T(8,128)(2,1)} %gout_hbm.1, ...), custom_call_target="tpu_custom_call" | custom-call | tf_op jit(solution)/shard_map/layer/pallas_call | solution.py:449
  38.0 5.4 %put_out.1 = (bf16[2,768,1024]{2,1,0:T(8,128)(2,1)}, bf16[2,768,1024]{2,1,0:T(8,128)(2,1)}, bf16[2,1024,1024]{2,1,0:T(8,128)(2,1)}, bf16[2,1024,1024]{2,1,0:T(8,128)(2,1)}, f32[32,64]{1,0:T(8,128)}) custom-call(bf16[2,768,1024]{2,1,0:T(8,128)(2,1)S(1)} %get-tuple-element.15.refs_0_, bf16[2,768,1024]{2,1,0:T(8,128)(2,1)S(1)} %get-tuple-element.16.refs_1_, ...), custom_call_target="tpu_custom_call" | custom-call | tf_op jit(solution)/shard_map/put_out/pallas_call | solution.py:505

commit v8 on v7

--- a/solution.py
+++ b/solution.py
@@ -12,6 +12,7 @@
 BF16 = jnp.bfloat16
 NT = (((1,), (1,)), ((), ()))
 VMEM_BYTES = 67043328
+SENDS = 16
 
 
 def dot(a, b):
@@ -40,12 +41,18 @@
         self.send_sem, self.recv_sem, self.groups = send_sem, recv_sem, []
 
     def group(self, whole):
+        if len(self.groups) >= SENDS:
+            self.sent(len(self.groups) - SENDS)
         self.groups.append(whole)
         return Group(self, len(self.groups) - 1, whole)
 
     def drain(self):
-        for i, whole in enumerate(self.groups):
-            pltpu.make_async_copy(whole, whole, self.send_sem.at[i]).wait()
+        for i in range(max(0, len(self.groups) - SENDS), len(self.groups)):
+            self.sent(i)
+
+    def sent(self, i):
+        whole = self.groups[i]
+        pltpu.make_async_copy(whole, whole, self.send_sem.at[i % SENDS]).wait()
 
 
 class Group:
@@ -56,7 +63,7 @@
         pltpu.make_async_remote_copy(
             src_ref=src,
             dst_ref=dst,
-            send_sem=self.net.send_sem.at[self.index],
+            send_sem=self.net.send_sem.at[self.index % SENDS],
             recv_sem=self.net.recv_sem.at[self.index],
             device_id=peer,
             device_id_type=MESH,
@@ -128,8 +135,12 @@
     far_peers = [(t, g * 2 + par) for t, g in there]
 
     load_rt = pltpu.make_async_copy(rt_hbm, rt, w_sem.at[0])
+    first = rows // 384 * 128
+    spans = [(0, pl.ds(0, first)), (0, pl.ds(first, rows - first))]
+    spans += [(c, pl.ds(0, rows)) for c in range(1, clips)]
     load_tok = [
-        pltpu.make_async_copy(tok_hbm.at[c], tok.at[c], w_sem.at[3 + clips + c]) for c in range(clips)
+        pltpu.make_async_copy(tok_hbm.at[at], tok.at[at], w_sem.at[2 + clips + i + 1])
+        for i, at in enumerate(spans)
     ]
     load_gout = [
         pltpu.make_async_copy(gout_hbm.at[c], gout.at[c], w_sem.at[1 + c]) for c in range(clips)
@@ -146,9 +157,10 @@
 
     load_rt.wait()
     values, peaks, masses = [], [], []
-    for c in range(clips):
-        load_tok[c].wait()
-        values.append(dot_nt(rt[...], tok[c]))
+    for load, at in zip(load_tok, spans):
+        load.wait()
+        values.append(dot_nt(rt[...], tok[at]))
+    values = [jnp.concatenate(values[:2], axis=1)] + values[2:]
     for c, value in enumerate(values):
         lg[c] = value
         peak = jnp.max(value, axis=1, keepdims=True)
@@ -493,8 +505,8 @@
             pltpu.VMEM((seq_n, half) + tile, BF16),
             pltpu.VMEM((seq_n, half) + tile, BF16),
             pltpu.VMEM((seq_n * half - 1,) + tile, BF16),
-            pltpu.SemaphoreType.DMA((2 * clips + 3,)),
-            pltpu.SemaphoreType.DMA((n_groups,)),
+            pltpu.SemaphoreType.DMA((2 * clips + 4,)),
+            pltpu.SemaphoreType.DMA((SENDS,)),
             pltpu.SemaphoreType.DMA((n_groups,)),
         ],
         compiler_params=pltpu.CompilerParams(

time: 43.6 us -> 43.1 us (0.989)
  Pallas kernels: 42.8 us -> 42.3 us
    pallas_call x1, Pallas kernels: 37.4 us -> 36.9 us  [on_device(): pl.pallas_call(functools.partial(layer, seq_n, exp_n), out_shape=outs, in...]
where the time goes in v8:
time: 43.1 us; the launch traced here: 42.9 us
  Pallas kernels  42.3 us (98%)
  between operations  0.64 us (1%)
    pallas_call x1, Pallas kernels, on_device(): pl.pallas_call(functools.partial(layer, seq_n, exp_n), out_shape=outs, in...  36.9 us
    pallas_call x1, Pallas kernels, on_device(): pl.pallas_call(functools.partial(put_out, len(outs)), out_shape=outs, in_...  5.39 us

profile of v8, /device:TPU:0, one launch (start us, length us, event | category | flops | bytes accessed | tf_op | source)
XLA Modules:
  0.0 42.9 jit_solution(606754967284967475)
XLA Ops:
  0.6 36.9 %layer.1 = (bf16[2,768,1024]{2,1,0:T(8,128)(2,1)S(1)}, bf16[2,768,1024]{2,1,0:T(8,128)(2,1)S(1)}, bf16[2,1024,1024]{2,1,0:T(8,128)(2,1)S(1)}, bf16[2,1024,1024]{2,1,0:T(8,128)(2,1)S(1)}, f32[32,64]{1,0:T(8,128)S(1)}) custom-call(bf16[2,768,1024]{2,1,0:T(8,128)(2,1)} %tok_hbm.1, bf16[64,1024]{1,0:T(8,128)(2,1)} %bitcast.1, bf16[2,768,1024]{2,1,0:T(8,128)(2,1)} %gout_hbm.1, ...), custom_call_target="tpu_custom_call" | custom-call | tf_op jit(solution)/shard_map/layer/pallas_call | solution.py:461
  37.5 5.4 %put_out.1 = (bf16[2,768,1024]{2,1,0:T(8,128)(2,1)}, bf16[2,768,1024]{2,1,0:T(8,128)(2,1)}, bf16[2,1024,1024]{2,1,0:T(8,128)(2,1)}, bf16[2,1024,1024]{2,1,0:T(8,128)(2,1)}, f32[32,64]{1,0:T(8,128)}) custom-call(bf16[2,768,1024]{2,1,0:T(8,128)(2,1)S(1)} %get-tuple-element.15.refs_0_, bf16[2,768,1024]{2,1,0:T(8,128)(2,1)S(1)} %get-tuple-element.16.refs_1_, ...), custom_call_target="tpu_custom_call" | custom-call | tf_op jit(solution)/shard_map/put_out/pallas_call | solution.py:517
